TPU v7x, 128 devices: a whole 4x4x4 slice. The times are simulated.
128 devices in a mesh: dp: 1, tp: 2 (over core), wg: 64 (over z, y, x).
Axes of the slice: x: 4, y: 4, z: 4, core: 2. Of those that a mesh axis runs over, the one named last changes fastest.
Arguments:
- hidden: bfloat16 [64, 1024, 1024], P(('dp', 'wg'))
- attn_mask: int32 [64, 1024], P(('dp', 'wg'))
- ln1_scale: bfloat16 [2, 1024], replicated
- ln1_bias: bfloat16 [2, 1024], replicated
- w_qkv: bfloat16 [2, 1024, 16, 3, 64], P(None, 'wg', 'tp')
- b_qkv: bfloat16 [2, 16, 3, 64], P(None, 'tp')
- w_out: bfloat16 [2, 16, 64, 1024], P(None, 'tp', None, 'wg')
- b_out: bfloat16 [2, 1024], replicated
- ln2_scale: bfloat16 [2, 1024], replicated
- ln2_bias: bfloat16 [2, 1024], replicated
- w_up: bfloat16 [2, 1024, 4096], P(None, 'wg', 'tp')
- b_up: bfloat16 [2, 4096], P(None, 'tp')
- w_down: bfloat16 [2, 4096, 1024], P(None, 'tp', 'wg')
- b_down: bfloat16 [2, 1024], replicated
Outputs:
- output 1: bfloat16 [64, 1024, 1024], P(('dp', 'wg'))
- output 2: bfloat16 [2, 64, 1024, 16, 64], P(None, ('dp', 'wg'), None, 'tp')
- output 3: bfloat16 [2, 64, 1024, 16, 64], P(None, ('dp', 'wg'), None, 'tp')
All inputs are finite; a program needn't handle non-finite values.
Results may differ from a plain program's by a relative error of at most 0.02.
Values are sent between devices in bfloat16 or wider.
A program may use at most 1 GiB of HBM per device.

v0:
```python
import math
import jax
import jax.numpy as jnp
from jax import lax
from jax.sharding import PartitionSpec as P

LN_EPS = 1e-5


def alibi_slopes(n_heads):
    closest = 2 ** int(math.floor(math.log2(n_heads)))
    slope_base = 2.0 ** (-8.0 / closest)
    slope_list = [slope_base ** (i + 1) for i in range(closest)]
    extra_base = 2.0 ** (-4.0 / closest)
    slope_list = slope_list + [extra_base ** (2 * i + 1) for i in range(n_heads - closest)]
    return jnp.array(slope_list, dtype=jnp.float32)


def layer_norm(values, ln_scale, ln_shift):
    as_float = values.astype(jnp.float32)
    mean_val = jnp.mean(as_float, axis=-1, keepdims=True)
    centered = as_float - mean_val
    variance = jnp.mean(centered * centered, axis=-1, keepdims=True)
    normed = centered * lax.rsqrt(variance + LN_EPS)
    return (normed * ln_scale.astype(jnp.float32) + ln_shift.astype(jnp.float32)).astype(jnp.bfloat16)


def add_residual(hidden, branch, bias):
    return (hidden.astype(jnp.float32) + branch.astype(jnp.float32) + bias.astype(jnp.float32)).astype(jnp.bfloat16)


def alibi_attention(qkv_out, attn_mask, slopes):
    seq_len = qkv_out.shape[1]
    head_dim = qkv_out.shape[-1]
    query_heads = qkv_out[:, :, :, 0]
    key_heads = qkv_out[:, :, :, 1]
    value_heads = qkv_out[:, :, :, 2]
    positions = jnp.maximum(jnp.cumsum(attn_mask, axis=1) - 1, 0).astype(jnp.float32)
    token_idx = jnp.arange(seq_len)
    causal = token_idx[None, :] <= token_idx[:, None]
    same_tok = token_idx[None, :] == token_idx[:, None]
    allowed = causal[None] & ((attn_mask[:, None, :] == 1) | same_tok[None])
    scores = jnp.einsum('bqnd,bknd->bnqk', query_heads, key_heads, preferred_element_type=jnp.float32) / math.sqrt(head_dim)
    rel_pos = positions[:, None, :] - positions[:, :, None]
    scores = scores + slopes[None, :, None, None] * rel_pos[:, None]
    scores = jnp.where(allowed[:, None], scores, -1e30)
    attn_probs = jax.nn.softmax(scores, axis=-1).astype(jnp.bfloat16)
    context = jnp.einsum('bnqk,bknd->bqnd', attn_probs, value_heads, preferred_element_type=jnp.float32).astype(jnp.bfloat16)
    return context, key_heads, value_heads


def solution(mesh):
    tp_size = mesh.shape['tp']
    batch_axes = ('dp', 'wg')

    def device_fn(hidden, attn_mask, ln1_scale, ln1_bias, w_qkv, b_qkv, w_out, b_out,
                  ln2_scale, ln2_bias, w_up, b_up, w_down, b_down):
        local_heads = w_qkv.shape[2]
        head_start = lax.axis_index('tp') * local_heads
        slopes = lax.dynamic_slice_in_dim(alibi_slopes(local_heads * tp_size), head_start, local_heads)
        key_list = []
        value_list = []
        for layer_idx in range(w_qkv.shape[0]):
            qkv_full = lax.all_gather(w_qkv[layer_idx], 'wg', axis=0, tiled=True)
            out_full = lax.all_gather(w_out[layer_idx], 'wg', axis=2, tiled=True)
            up_full = lax.all_gather(w_up[layer_idx], 'wg', axis=0, tiled=True)
            down_full = lax.all_gather(w_down[layer_idx], 'wg', axis=1, tiled=True)
            normed = layer_norm(hidden, ln1_scale[layer_idx], ln1_bias[layer_idx])
            qkv_out = jnp.einsum('bsh,hntd->bsntd', normed, qkv_full, preferred_element_type=jnp.float32)
            qkv_out = (qkv_out + b_qkv[layer_idx].astype(jnp.float32)).astype(jnp.bfloat16)
            context, key_heads, value_heads = alibi_attention(qkv_out, attn_mask, slopes)
            attn_part = jnp.einsum('bsnd,ndh->bsh', context, out_full, preferred_element_type=jnp.float32).astype(jnp.bfloat16)
            attn_sum = lax.psum(attn_part, 'tp')
            mid_hidden = add_residual(hidden, attn_sum, b_out[layer_idx])
            normed_mlp = layer_norm(mid_hidden, ln2_scale[layer_idx], ln2_bias[layer_idx])
            up_pre = jnp.einsum('bsh,hf->bsf', normed_mlp, up_full, preferred_element_type=jnp.float32)
            up_act = jax.nn.gelu(up_pre + b_up[layer_idx].astype(jnp.float32), approximate=True).astype(jnp.bfloat16)
            down_part = jnp.einsum('bsf,fh->bsh', up_act, down_full, preferred_element_type=jnp.float32).astype(jnp.bfloat16)
            down_sum = lax.psum(down_part, 'tp')
            hidden = add_residual(mid_hidden, down_sum, b_down[layer_idx])
            key_list.append(key_heads)
            value_list.append(value_heads)
        return hidden, jnp.stack(key_list), jnp.stack(value_list)

    replicated = P(None, None)
    in_specs = (P(batch_axes, None, None), P(batch_axes, None), replicated, replicated,
                P(None, 'wg', 'tp', None, None), P(None, 'tp', None, None), P(None, 'tp', None, 'wg'), replicated,
                replicated, replicated, P(None, 'wg', 'tp'), P(None, 'tp'), P(None, 'tp', 'wg'), replicated)
    cache_spec = P(None, batch_axes, None, 'tp', None)
    out_specs = (P(batch_axes, None, None), cache_spec, cache_spec)
    return jax.shard_map(device_fn, mesh=mesh, in_specs=in_specs, out_specs=out_specs, check_vma=False)
```

profile of v0, /device:TPU:1, one launch (start us, length us, event | category | flops | bytes accessed | tf_op | source)
XLA Modules:
  0.0 798.8 jit_solution(16978623194841780184)
XLA Ops:
  16.9 2.4 broadcast_subtract_fusion
  20.7 57.1 %all-gather.19.cloned.1.call-done = bf16[1,8,64,1024]{2,1,0,3:T(8,128)(2,1)} async-done(((bf16[1,8,64,16]{2,1,0,3:T(8,128)(2,1)}), bf16[1,8,64,1024]{2,1,0,3:T(8,128)(2,1)}) %all-gather.19.cloned.1.call-update) | async-done | bytes 1048592 | tf_op jit(solution)/shard_map/all_gather | solution.py:65
  77.7 2.7 copy.42
  80.4 71.7 %all-gather.17.cloned.1.call-done = bf16[1,1024,8,3,64]{4,2,3,0,1:T(8,128)(2,1)} async-done(((bf16[1,16,8,3,64]{4,2,3,0,1:T(8,128)(2,1)}), bf16[1,1024,8,3,64]{4,2,3,0,1:T(8,128)(2,1)}) %all-gather.17.cloned.1.call-update) | async-done | bytes 3145744 | tf_op jit(solution)/shard_map/all_gather | solution.py:64
  152.1 7.6 copy.37
  159.7 5.6 fusion.100
  167.4 21.3 %fusion.192 = (f32[8,1024]{1,0:T(8,128)S(1)}, f32[8,1024,1024]{1,2,0:T(8,128)}) fusion(f32[1024,1024]{0,1:T(8,128)} %broadcast_subtract_fusion, f32[8]{0:T(128)S(1)} %dynamic_slice.3, pred[1024,1024]{0,1:T(8,128)(4,1)} %fusion.91, bf16[1,1024,8,3,64]{1,4,3,2,0:T(8,128)(2,1)} %fusion.97), kind=kOutput, calls=%fused_computation.218 | convolution fusion | flops 1124074496 | bytes 40927264 | tf_op jit(solution)/shard_map/sub | solution.py:47
  188.7 14.8 %fusion.133 = bf16[1,1024,1024]{2,1,0:T(8,128)(2,1)} fusion(f32[8,1024,1024]{1,2,0:T(8,128)} %get-tuple-element.38, f32[8,1024]{1,0:T(8,128)S(1)} %get-tuple-element.37, bf16[1,8,64,1024]{3,2,1,0:T(8,128)(2,1)S(1)} %copy.42, bf16[1,1024,8,3,64]{1,4,3,2,0:T(8,128)(2,1)} %fusion.97), kind=kOutput, calls=%fused_computation.142 | convolution fusion | flops 2165833728 | bytes 37781504 | tf_op jit(solution)/shard_map/bsnd,ndh->bsh/dot_general | solution.py:72
  206.9 23.2 %all-reduce.5.cloned.1.call-done = bf16[1,1024,1024]{2,1,0:T(8,128)(2,1)} async-done(((bf16[1,1024,1024]{2,1,0:T(8,128)(2,1)}), bf16[1,1024,1024]{2,1,0:T(8,128)(2,1)}) %all-reduce.5.cloned.1.call-update) | async-done | bytes 2097168 | tf_op jit(solution)/shard_map/psum | solution.py:73
  230.1 2.4 convert_reduce_fusion.2
  234.5 65.7 %all-gather.21.cloned.1.call-done = bf16[1,1024,2048]{2,1,0:T(8,128)(2,1)} async-done(((bf16[1,16,2048]{2,1,0:T(8,128)(2,1)}), bf16[1,1024,2048]{2,1,0:T(8,128)(2,1)}) %all-gather.21.cloned.1.call-update) | async-done | bytes 4194320 | tf_op jit(solution)/shard_map/all_gather | solution.py:66
  300.2 10.7 %fusion.79 = f32[1024,2048]{1,0:T(8,128)} fusion(bf16[1,1024,2048]{2,1,0:T(8,128)(2,1)} %all-gather.21.cloned.1.call-done, bf16[1,1024,1024]{2,1,0:T(8,128)(2,1)} %copy-done.1, f32[1024]{0:T(1024)S(1)} %bitcast.201, f32[1024]{0:T(1024)S(1)} %bitcast.199, f32[1024]{0:T(1024)S(1)} %add_rsqrt_fusion.2, f32[1024]{0:T(1024)S(1)} %broadcast_multiply_fusion.2), kind=kOutput, calls=%fused_computation.96 | convolution fusion | flops 4301258752 | bytes 14696448 | tf_op jit(solution)/shard_map/bsh,hf->bsf/dot_general | solution.py:76
  310.9 58.6 %all-gather.23.cloned.1.call-done = bf16[1,2048,1024]{1,2,0:T(8,128)(2,1)} async-done(((bf16[1,2048,16]{1,2,0:T(8,128)(2,1)}), bf16[1,2048,1024]{1,2,0:T(8,128)(2,1)}) %all-gather.23.cloned.1.call-update) | async-done | bytes 4194320 | tf_op jit(solution)/shard_map/all_gather | solution.py:67
  369.5 11.3 %convert_bitcast_fusion.1 = bf16[1,1024,1024]{2,1,0:T(8,128)(2,1)} fusion(bf16[1,2048,1024]{1,2,0:T(8,128)(2,1)} %all-gather.23.cloned.1.call-done, f32[1024,2048]{1,0:T(8,128)} %fusion.79, f32[2048]{0:T(1024)S(1)} %bitcast.193), kind=kOutput, calls=%fused_computation.132 | convolution fusion | flops 4316987392 | bytes 14688256 | tf_op jit(solution)/shard_map/bsf,fh->bsh/dot_general | solution.py:78
  381.3 53.5 %all-gather.27.cloned.1.call-done = bf16[1,8,64,1024]{2,1,0,3:T(8,128)(2,1)} async-done(((bf16[1,8,64,16]{2,1,0,3:T(8,128)(2,1)}), bf16[1,8,64,1024]{2,1,0,3:T(8,128)(2,1)}) %all-gather.27.cloned.1.call-update) | async-done | bytes 1048592 | tf_op jit(solution)/shard_map/all_gather | solution.py:65
  434.8 2.5 copy.48
  437.3 71.2 %all-gather.25.cloned.1.call-done = bf16[1,1024,8,3,64]{4,2,3,0,1:T(8,128)(2,1)} async-done(((bf16[1,16,8,3,64]{4,2,3,0,1:T(8,128)(2,1)}), bf16[1,1024,8,3,64]{4,2,3,0,1:T(8,128)(2,1)}) %all-gather.25.cloned.1.call-update) | async-done | bytes 3145744 | tf_op jit(solution)/shard_map/all_gather | solution.py:64
  508.6 7.7 copy.44
  516.3 21.7 %all-reduce.7.cloned.1.call-done = bf16[1,1024,1024]{2,1,0:T(8,128)(2,1)} async-done(((bf16[1,1024,1024]{2,1,0:T(8,128)(2,1)}), bf16[1,1024,1024]{2,1,0:T(8,128)(2,1)}) %all-reduce.7.cloned.1.call-update) | async-done | bytes 2097168 | tf_op jit(solution)/shard_map/psum | solution.py:79
  538.0 3.2 convert_reduce_fusion.1
  541.9 3.8 fusion.105
  547.8 21.3 %fusion.197 = (f32[8,1024]{1,0:T(8,128)S(1)}, f32[8,1024,1024]{1,2,0:T(8,128)}) fusion(f32[1024,1024]{0,1:T(8,128)} %broadcast_subtract_fusion, f32[8]{0:T(128)S(1)} %dynamic_slice.3, pred[1024,1024]{0,1:T(8,128)(4,1)} %fusion.91, bf16[1,1024,8,3,64]{1,4,2,3,0:T(8,128)(2,1)} %fusion.98), kind=kOutput, calls=%fused_computation.219 | convolution fusion | flops 1124074496 | bytes 40927264 | tf_op jit(solution)/shard_map/sub | solution.py:47
  569.0 14.7 %fusion.134 = bf16[1,1024,1024]{2,1,0:T(8,128)(2,1)} fusion(f32[8,1024,1024]{1,2,0:T(8,128)} %get-tuple-element.40, f32[8,1024]{1,0:T(8,128)S(1)} %get-tuple-element.39, bf16[1,8,64,1024]{3,2,1,0:T(8,128)(2,1)S(1)} %copy.48, bf16[1,1024,8,3,64]{1,4,2,3,0:T(8,128)(2,1)} %fusion.98), kind=kOutput, calls=%fused_computation.143 | convolution fusion | flops 2165833728 | bytes 37781504 | tf_op jit(solution)/shard_map/bsnd,ndh->bsh/dot_general | solution.py:72
  585.3 26.0 %all-reduce.9.cloned.1.call-done = bf16[1,1024,1024]{2,1,0:T(8,128)(2,1)} async-done(((bf16[1,1024,1024]{2,1,0:T(8,128)(2,1)}), bf16[1,1024,1024]{2,1,0:T(8,128)(2,1)}) %all-reduce.9.cloned.1.call-update) | async-done | bytes 2097168 | tf_op jit(solution)/shard_map/psum | solution.py:73
  611.4 2.4 convert_reduce_fusion
  615.8 65.6 %all-gather.29.cloned.1.call-done = bf16[1,1024,2048]{2,1,0:T(8,128)(2,1)} async-done(((bf16[1,16,2048]{2,1,0:T(8,128)(2,1)}), bf16[1,1024,2048]{2,1,0:T(8,128)(2,1)}) %all-gather.29.cloned.1.call-update) | async-done | bytes 4194320 | tf_op jit(solution)/shard_map/all_gather | solution.py:66
  681.5 10.7 %fusion.75 = f32[1024,2048]{1,0:T(8,128)} fusion(bf16[1,1024,2048]{2,1,0:T(8,128)(2,1)} %all-gather.29.cloned.1.call-done, bf16[1,1024,1024]{2,1,0:T(8,128)(2,1)} %copy-done.2, f32[1024]{0:T(1024)S(1)} %bitcast.197, f32[1024]{0:T(1024)S(1)} %bitcast.196, f32[1024]{0:T(1024)S(1)} %add_rsqrt_fusion, f32[1024]{0:T(1024)S(1)} %broadcast_multiply_fusion), kind=kOutput, calls=%fused_computation.91 | convolution fusion | flops 4301258752 | bytes 14696448 | tf_op jit(solution)/shard_map/bsh,hf->bsf/dot_general | solution.py:76
  692.2 58.2 %all-gather.31.cloned.1.call-done = bf16[1,2048,1024]{1,2,0:T(8,128)(2,1)} async-done(((bf16[1,2048,16]{1,2,0:T(8,128)(2,1)}), bf16[1,2048,1024]{1,2,0:T(8,128)(2,1)}) %all-gather.31.cloned.1.call-update) | async-done | bytes 4194320 | tf_op jit(solution)/shard_map/all_gather | solution.py:67
  750.3 11.3 %convert_bitcast_fusion = bf16[1,1024,1024]{2,1,0:T(8,128)(2,1)} fusion(bf16[1,2048,1024]{1,2,0:T(8,128)(2,1)} %all-gather.31.cloned.1.call-done, f32[1024,2048]{1,0:T(8,128)} %fusion.75, f32[2048]{0:T(1024)S(1)} %bitcast.192), kind=kOutput, calls=%fused_computation.123 | convolution fusion | flops 4316987392 | bytes 14688256 | tf_op jit(solution)/shard_map/bsf,fh->bsh/dot_general | solution.py:78
  765.2 2.4 pad_maximum_fusion
  767.6 20.3 %all-reduce.11.cloned.1.call-done = bf16[1,1024,1024]{2,1,0:T(8,128)(2,1)} async-done(((bf16[1,1024,1024]{2,1,0:T(8,128)(2,1)}), bf16[1,1024,1024]{2,1,0:T(8,128)(2,1)}) %all-reduce.11.cloned.1.call-update) | async-done | bytes 2097168 | tf_op jit(solution)/shard_map/psum | solution.py:79
  787.9 3.9 fusion.72
  (93 shorter events, 28.5 us)
Async XLA Ops:
  7.2 8.9 %copy-start = (bf16[1,1024,1024]{2,1,0:T(8,128)(2,1)S(1)}, bf16[1,1024,1024]{2,1,0:T(8,128)(2,1)}, u32[]{:S(2)}) copy-start(bf16[1,1024,1024]{2,1,0:T(8,128)(2,1)} %param.15) | copy-start | bytes 6291460
  7.2 9.6 %copy-start.8 = (bf16[2,1024]{1,0:T(2,128)(2,1)S(1)}, bf16[2,1024]{1,0:T(2,128)(2,1)}, u32[]{:S(2)}) copy-start(bf16[2,1024]{1,0:T(2,128)(2,1)} %param.17) | copy-start | bytes 12292
  7.2 9.6 %copy-start.9 = (bf16[2,1024]{1,0:T(2,128)(2,1)S(1)}, bf16[2,1024]{1,0:T(2,128)(2,1)}, u32[]{:S(2)}) copy-start(bf16[2,1024]{1,0:T(2,128)(2,1)} %param.18) | copy-start | bytes 12292
  7.2 70.6 %all-gather.19.cloned.1.call-start = ((), (), s32[]{:S(2)}) async-start(), calls=%async_computation.5 | async-start | bytes 2129920 | tf_op jit(solution)/shard_map/all_gather | solution.py:65
  8.8 143.3 %all-gather.17.cloned.1.call-start = ((), (), s32[]{:S(2)}) async-start(), calls=%async_computation.4 | async-start | bytes 6389760 | tf_op jit(solution)/shard_map/all_gather | solution.py:64
  10.5 219.6 %all-reduce.5.cloned.1.call-start = ((), (), s32[]{:S(2)}) async-start(), calls=%async_computation | async-start | bytes 4194304 | tf_op jit(solution)/shard_map/psum | solution.py:73
  188.7 15.0 %copy-start.5 = (bf16[2,16,2048]{2,1,0:T(8,128)(2,1)S(1)}, bf16[2,16,2048]{2,1,0:T(8,128)(2,1)}, u32[]{:S(2)}) copy-start(bf16[2,16,2048]{2,1,0:T(8,128)(2,1)} %param.25) | copy-start | bytes 393220
  188.7 15.7 %copy-start.6 = (bf16[2,2048,16]{1,2,0:T(8,128)(2,1)S(1)}, bf16[2,2048,16]{1,2,0:T(8,128)(2,1)}, u32[]{:S(2)}) copy-start(bf16[2,2048,16]{1,2,0:T(8,128)(2,1)} %param.27) | copy-start | bytes 393220
  188.7 18.1 %copy-start.10 = (bf16[2,1024]{1,0:T(2,128)(2,1)S(1)}, bf16[2,1024]{1,0:T(2,128)(2,1)}, u32[]{:S(2)}) copy-start(bf16[2,1024]{1,0:T(2,128)(2,1)} %param.22) | copy-start | bytes 12292
  188.7 18.1 %copy-start.11 = (bf16[2,1024]{1,0:T(2,128)(2,1)S(1)}, bf16[2,1024]{1,0:T(2,128)(2,1)}, u32[]{:S(2)}) copy-start(bf16[2,1024]{1,0:T(2,128)(2,1)} %param.23) | copy-start | bytes 12292
  188.7 18.1 %copy-start.12 = (bf16[2,1024]{1,0:T(2,128)(2,1)S(1)}, bf16[2,1024]{1,0:T(2,128)(2,1)}, u32[]{:S(2)}) copy-start(bf16[2,1024]{1,0:T(2,128)(2,1)} %param.24) | copy-start | bytes 12292
  188.7 18.1 %copy-start.7 = (bf16[2,2048]{1,0:T(2,128)(2,1)S(1)}, bf16[2,2048]{1,0:T(2,128)(2,1)}, u32[]{:S(2)}) copy-start(bf16[2,2048]{1,0:T(2,128)(2,1)} %param.26) | copy-start | bytes 24580
  203.6 96.6 %all-gather.21.cloned.1.call-start = ((), (), s32[]{:S(2)}) async-start(), calls=%async_computation.6 | async-start | bytes 4259840 | tf_op jit(solution)/shard_map/all_gather | solution.py:66
  204.4 165.1 %all-gather.23.cloned.1.call-start = ((), (), s32[]{:S(2)}) async-start(), calls=%async_computation.7 | async-start | bytes 4259840 | tf_op jit(solution)/shard_map/all_gather | solution.py:67
  205.1 229.7 %all-gather.27.cloned.1.call-start = ((), (), s32[]{:S(2)}) async-start(), calls=%async_computation.9 | async-start | bytes 2129920 | tf_op jit(solution)/shard_map/all_gather | solution.py:65
  205.8 302.8 %all-gather.25.cloned.1.call-start = ((), (), s32[]{:S(2)}) async-start(), calls=%async_computation.8 | async-start | bytes 6389760 | tf_op jit(solution)/shard_map/all_gather | solution.py:64
  206.5 331.4 %all-reduce.7.cloned.1.call-start = ((), (), s32[]{:S(2)}) async-start(), calls=%async_computation.1 | async-start | bytes 4194304 | tf_op jit(solution)/shard_map/psum | solution.py:79
  232.5 1.3 copy-start.1
  369.5 11.8 %copy-start.13 = (bf16[2,1024]{1,0:T(2,128)(2,1)S(1)}, bf16[2,1024]{1,0:T(2,128)(2,1)}, u32[]{:S(2)}) copy-start(bf16[2,1024]{1,0:T(2,128)(2,1)} %param.28) | copy-start | bytes 12292
  380.8 230.6 %all-reduce.9.cloned.1.call-start = ((), (), s32[]{:S(2)}) async-start(), calls=%async_computation.2 | async-start | bytes 4194304 | tf_op jit(solution)/shard_map/psum | solution.py:73
  537.9 3.9 copy-start.4
  583.8 97.7 %all-gather.29.cloned.1.call-start = ((), (), s32[]{:S(2)}) async-start(), calls=%async_computation.10 | async-start | bytes 4259840 | tf_op jit(solution)/shard_map/all_gather | solution.py:66
  584.4 166.0 %all-gather.31.cloned.1.call-start = ((), (), s32[]{:S(2)}) async-start(), calls=%async_computation.11 | async-start | bytes 4259840 | tf_op jit(solution)/shard_map/all_gather | solution.py:67
  585.1 202.8 %all-reduce.11.cloned.1.call-start = ((), (), s32[]{:S(2)}) async-start(), calls=%async_computation.3 | async-start | bytes 4194304 | tf_op jit(solution)/shard_map/psum | solution.py:79
  613.8 1.3 copy-start.2
  765.2 22.7 %copy-start.3 = (bf16[1,1024,1024]{2,1,0:T(8,128)(2,1)S(1)}, bf16[1,1024,1024]{2,1,0:T(8,128)(2,1)}, u32[]{:S(2)}) copy-start(bf16[1,1024,1024]{2,1,0:T(8,128)(2,1)} %copy-done.2) | copy-start | bytes 6291460
Sparse Core Ops, SparseCore 0:
  11.4 66.2 all-gather.18
  81.1 70.9 all-gather.16
  203.7 26.3 all-reduce.4
  232.8 67.3 all-gather.20
  303.5 65.9 all-gather.22
  372.2 62.5 all-gather.26
  437.6 70.9 all-gather.24
  511.6 26.3 all-reduce.6
  583.9 27.4 all-reduce.8
  614.1 67.3 all-gather.28
  684.3 65.9 all-gather.30
  761.8 26.0 all-reduce.10
where the time goes:
time: 802 us; the launch traced here: 799 us
  waiting for transfers between devices  595 us (74%)
  matrix products  126 us (16%)
  local copies, waits for them, and re-layouts  32.8 us (4%)
  other arithmetic  29.6 us (4%)
  between operations  14.7 us (2%)
    all_gather x2, waiting for transfers between devices, device_fn(): qkv_full = lax.all_gather(w_qkv[layer_idx], 'wg', axis=0, tiled=True)  143 us
    all_gather x2, waiting for transfers between devices, device_fn(): up_full = lax.all_gather(w_up[layer_idx], 'wg', axis=0, tiled=True)  131 us
    all_gather x2, waiting for transfers between devices, device_fn(): down_full = lax.all_gather(w_down[layer_idx], 'wg', axis=1, tiled=True)  117 us
    all_gather x2, waiting for transfers between devices, device_fn(): out_full = lax.all_gather(w_out[layer_idx], 'wg', axis=2, tiled=True)  111 us
    psum x2, waiting for transfers between devices, device_fn(): attn_sum = lax.psum(attn_part, 'tp')  49.2 us
    sub x2, matrix products, alibi_attention(): attn_probs = jax.nn.softmax(scores, axis=-1).astype(jnp.bfloat16)  42.6 us
    psum x2, waiting for transfers between devices, device_fn(): down_sum = lax.psum(down_part, 'tp')  42 us
    dot_general x2, matrix products, device_fn(): jnp.einsum('bsnd,ndh->bsh', context, out_full, preferred_element_type=jnp...  29.6 us
  transfers between devices with their start and end apart: 12, of which 12 were waited for; matrix products, arithmetic and copies ran while one was open for 9% of the time, Pallas kernels for 0%

commit v1 on v0

--- a/solution.py
+++ b/solution.py
@@ -2,9 +2,16 @@
 import jax
 import jax.numpy as jnp
 from jax import lax
+from jax.experimental import pallas as pl
+from jax.experimental.pallas import tpu as pltpu
 from jax.sharding import PartitionSpec as P
 
 LN_EPS = 1e-5
+MESH = pl.DeviceIdType.MESH
+UNITS = 24
+CHUNKS = 16
+STAGES = 6
+ORDERS = (('x', 'y', 'z'), ('y', 'z', 'x'), ('z', 'x', 'y'))
 
 
 def alibi_slopes(n_heads):
@@ -29,12 +36,9 @@
     return (hidden.astype(jnp.float32) + branch.astype(jnp.float32) + bias.astype(jnp.float32)).astype(jnp.bfloat16)
 
 
-def alibi_attention(qkv_out, attn_mask, slopes):
-    seq_len = qkv_out.shape[1]
-    head_dim = qkv_out.shape[-1]
-    query_heads = qkv_out[:, :, :, 0]
-    key_heads = qkv_out[:, :, :, 1]
-    value_heads = qkv_out[:, :, :, 2]
+def alibi_attention(query_heads, key_heads, value_heads, attn_mask, slopes):
+    seq_len = query_heads.shape[1]
+    head_dim = query_heads.shape[-1]
     positions = jnp.maximum(jnp.cumsum(attn_mask, axis=1) - 1, 0).astype(jnp.float32)
     token_idx = jnp.arange(seq_len)
     causal = token_idx[None, :] <= token_idx[:, None]
@@ -45,8 +49,129 @@
     scores = scores + slopes[None, :, None, None] * rel_pos[:, None]
     scores = jnp.where(allowed[:, None], scores, -1e30)
     attn_probs = jax.nn.softmax(scores, axis=-1).astype(jnp.bfloat16)
-    context = jnp.einsum('bnqk,bknd->bqnd', attn_probs, value_heads, preferred_element_type=jnp.float32).astype(jnp.bfloat16)
-    return context, key_heads, value_heads
+    return jnp.einsum('bnqk,bknd->bqnd', attn_probs, value_heads, preferred_element_type=jnp.float32).astype(jnp.bfloat16)
+
+
+class Torus:
+    def __init__(self, blocks, send_sem, recv_sem):
+        self.blocks, self.send_sem, self.recv_sem = blocks, send_sem, recv_sem
+        me = lax.axis_index('wg')
+        self.pos = {'z': lax.div(me, 16), 'y': lax.rem(lax.div(me, 4), 4), 'x': lax.rem(me, 4)}
+        self.next = {ax: lax.rem(p + 1, 4) for ax, p in self.pos.items()}
+        self.prev = {ax: lax.rem(p + 3, 4) for ax, p in self.pos.items()}
+        self.right = {ax: self.device({**self.pos, ax: self.next[ax]}) for ax in 'zyx'}
+        self.left = {ax: self.device({**self.pos, ax: self.prev[ax]}) for ax in 'zyx'}
+
+    @staticmethod
+    def device(pos):
+        return pos['z'] * 16 + pos['y'] * 4 + pos['x']
+
+    def view(self, unit, where, cols=None):
+        ref = self.blocks.at[unit, where['z'], where['y'], where['x']]
+        return ref if cols is None else self.blocks.at[unit, where['z'], where['y'], where['x'], :, cols]
+
+    def barrier(self):
+        sem = pltpu.get_barrier_semaphore()
+        for ax in 'zyx':
+            for dev in (self.left[ax], self.right[ax]):
+                pl.semaphore_signal(sem, inc=1, device_id={'wg': dev}, device_id_type=MESH)
+        pl.semaphore_wait(sem, 6)
+
+    def sends(self, chunk, stage):
+        every, low, high = slice(None), slice(0, 2), slice(2, 4)
+        out = []
+        for color, (a, b, c) in enumerate(ORDERS):
+            unit = 3 * chunk + color
+            if stage == 0:
+                here = dict(self.pos)
+                out += [(self.view(unit, here), self.right[a]), (self.view(unit, here), self.left[a])]
+            elif stage == 1:
+                out += [(self.view(unit, {**self.pos, a: self.prev[a]}, slice(0, 128)), self.right[a]),
+                        (self.view(unit, {**self.pos, a: self.next[a]}, slice(128, 256)), self.left[a])]
+            elif stage == 2:
+                row = {**self.pos, a: every}
+                out += [(self.view(unit, row), self.right[b]), (self.view(unit, row), self.left[b])]
+            elif stage == 3:
+                out += [(self.view(unit, {a: low, b: self.prev[b], c: self.pos[c]}), self.right[b]),
+                        (self.view(unit, {a: high, b: self.next[b], c: self.pos[c]}), self.left[b])]
+            elif stage == 4:
+                plane = {a: every, b: every, c: self.pos[c]}
+                out += [(self.view(unit, plane), self.right[c]), (self.view(unit, plane), self.left[c])]
+            else:
+                slow, fast = (a, b) if 'zyx'.index(a) < 'zyx'.index(b) else (b, a)
+                out += [(self.view(unit, {slow: low, fast: every, c: self.prev[c]}), self.right[c]),
+                        (self.view(unit, {slow: high, fast: every, c: self.next[c]}), self.left[c])]
+        return out
+
+    def start(self, chunk, stage):
+        for ref, dev in self.sends(chunk, stage):
+            pltpu.make_async_remote_copy(
+                src_ref=ref, dst_ref=ref, send_sem=self.send_sem.at[chunk, stage], recv_sem=self.recv_sem.at[chunk, stage],
+                device_id={'wg': dev}, device_id_type=MESH).start()
+
+    def wait(self, sem, chunk, stage):
+        w = self.blocks
+        size = (w.at[0:3, 0, 0, 0:2], w.at[0:3, 0, 0, 0], w.at[0:3, 0, 0:2], w.at[0:3, 0, 0], w.at[0:3, 0:2], w.at[0:3, 0])[stage]
+        pltpu.make_async_copy(size, size, sem.at[chunk, stage]).wait()
+
+    def step(self, chunk, stage):
+        if stage > 0:
+            self.wait(self.recv_sem, chunk, stage - 1)
+        if stage < STAGES:
+            self.start(chunk, stage)
+
+
+def gather_kernel(local_ref, blocks, send_sem, recv_sem, own_sem):
+    torus = Torus(blocks, send_sem, recv_sem)
+    own = pltpu.make_async_copy(local_ref, blocks.at[:, torus.pos['z'], torus.pos['y'], torus.pos['x']], own_sem)
+    own.start()
+    torus.barrier()
+    own.wait()
+    spacing = 2
+
+    def tick(t, carry):
+        for stage in reversed(range(STAGES + 1)):
+            chunk = t - spacing * stage
+
+            @pl.when((chunk >= 0) & (chunk < CHUNKS))
+            def _():
+                torus.step(chunk, stage)
+        return carry
+
+    lax.fori_loop(0, CHUNKS + spacing * STAGES, tick, 0)
+
+    def drain(chunk, carry):
+        for stage in range(STAGES):
+            torus.wait(send_sem, chunk, stage)
+        return carry
+
+    lax.fori_loop(0, CHUNKS, drain, 0)
+
+
+def gather_weights(local):
+    return pl.pallas_call(
+        gather_kernel,
+        out_shape=jax.ShapeDtypeStruct((2 * UNITS, 4, 4, 4, 16, 256), jnp.bfloat16),
+        in_specs=[pl.BlockSpec(memory_space=pl.ANY)],
+        out_specs=pl.BlockSpec(memory_space=pl.ANY),
+        scratch_shapes=[
+            pltpu.SemaphoreType.DMA((CHUNKS, STAGES)),
+            pltpu.SemaphoreType.DMA((CHUNKS, STAGES)),
+            pltpu.SemaphoreType.DMA,
+        ],
+        compiler_params=pltpu.CompilerParams(collective_id=0, has_side_effects=True),
+        name='torus_gather',
+    )(local)
+
+
+def pack_local(w_qkv, w_out, w_up, w_down):
+    def units(w):
+        return w.reshape(w.shape[0], 16, -1, 256).transpose(0, 2, 1, 3)
+    qkv = units(w_qkv.transpose(0, 1, 3, 2, 4))
+    out = units(w_out.reshape(w_out.shape[0], -1, 16).transpose(0, 2, 1))
+    up = units(w_up)
+    down = units(w_down.transpose(0, 2, 1))
+    return jnp.concatenate([qkv, out, up, down], axis=1).reshape(-1, 16, 256)
 
 
 def solution(mesh):
@@ -58,24 +183,24 @@
         local_heads = w_qkv.shape[2]
         head_start = lax.axis_index('tp') * local_heads
         slopes = lax.dynamic_slice_in_dim(alibi_slopes(local_heads * tp_size), head_start, local_heads)
+        blocks = gather_weights(pack_local(w_qkv, w_out, w_up, w_down)).reshape(2, UNITS, 1024, 256)
         key_list = []
         value_list = []
         for layer_idx in range(w_qkv.shape[0]):
-            qkv_full = lax.all_gather(w_qkv[layer_idx], 'wg', axis=0, tiled=True)
-            out_full = lax.all_gather(w_out[layer_idx], 'wg', axis=2, tiled=True)
-            up_full = lax.all_gather(w_up[layer_idx], 'wg', axis=0, tiled=True)
-            down_full = lax.all_gather(w_down[layer_idx], 'wg', axis=1, tiled=True)
+            w = blocks[layer_idx]
             normed = layer_norm(hidden, ln1_scale[layer_idx], ln1_bias[layer_idx])
-            qkv_out = jnp.einsum('bsh,hntd->bsntd', normed, qkv_full, preferred_element_type=jnp.float32)
-            qkv_out = (qkv_out + b_qkv[layer_idx].astype(jnp.float32)).astype(jnp.bfloat16)
-            context, key_heads, value_heads = alibi_attention(qkv_out, attn_mask, slopes)
-            attn_part = jnp.einsum('bsnd,ndh->bsh', context, out_full, preferred_element_type=jnp.float32).astype(jnp.bfloat16)
+            qkv_out = jnp.einsum('bsh,uhc->bsuc', normed, w[0:6], preferred_element_type=jnp.float32)
+            qkv_out = qkv_out.reshape(1, 1024, 3, local_heads, 64)
+            qkv_out = (qkv_out + b_qkv[layer_idx].transpose(1, 0, 2).astype(jnp.float32)).astype(jnp.bfloat16)
+            key_heads, value_heads = qkv_out[:, :, 1], qkv_out[:, :, 2]
+            context = alibi_attention(qkv_out[:, :, 0], key_heads, value_heads, attn_mask, slopes)
+            attn_part = jnp.einsum('bsuc,uhc->bsh', context.reshape(1, 1024, 2, 256), w[6:8], preferred_element_type=jnp.float32).astype(jnp.bfloat16)
             attn_sum = lax.psum(attn_part, 'tp')
             mid_hidden = add_residual(hidden, attn_sum, b_out[layer_idx])
             normed_mlp = layer_norm(mid_hidden, ln2_scale[layer_idx], ln2_bias[layer_idx])
-            up_pre = jnp.einsum('bsh,hf->bsf', normed_mlp, up_full, preferred_element_type=jnp.float32)
-            up_act = jax.nn.gelu(up_pre + b_up[layer_idx].astype(jnp.float32), approximate=True).astype(jnp.bfloat16)
-            down_part = jnp.einsum('bsf,fh->bsh', up_act, down_full, preferred_element_type=jnp.float32).astype(jnp.bfloat16)
+            up_pre = jnp.einsum('bsh,uhc->bsuc', normed_mlp, w[8:16], preferred_element_type=jnp.float32)
+            up_act = jax.nn.gelu(up_pre + b_up[layer_idx].reshape(8, 256).astype(jnp.float32), approximate=True).astype(jnp.bfloat16)
+            down_part = jnp.einsum('bsuc,uhc->bsh', up_act, w[16:24], preferred_element_type=jnp.float32).astype(jnp.bfloat16)
             down_sum = lax.psum(down_part, 'tp')
             hidden = add_residual(mid_hidden, down_sum, b_down[layer_idx])
             key_list.append(key_heads)

time: 802 us -> 406 us (0.51)
  waiting for transfers between devices: 595 us -> 89.5 us
  Pallas kernels: 0 us -> 116 us
    all_gather x8 -> x0, waiting for transfers between devices: 502 us -> none  [the longest x2 143 us: device_fn(): qkv_full = lax.all_gather(w_qkv[layer_idx], 'wg', axis=0, tiled=True)]
    pallas_call x0 -> x1, Pallas kernels: none -> 116 us  [gather_weights(): pl.pallas_call(gather_kernel, out_shape=jax.ShapeDtypeStruct((2 * UNITS,...]
    all_gather x4 -> x0, local copies, waits for them, and re-layouts: 20.5 us -> none  [the longest x2 15.3 us: device_fn(): qkv_full = lax.all_gather(w_qkv[layer_idx], 'wg', axis=0, tiled=True)]
    slice x4, local copies, waits for them, and re-layouts: 2.42 us -> 22.7 us  [the longest x1 12.5 us: device_fn(): w[8:16]]
    unnamed x2 -> x0, matrix products: 9.42 us -> none
    dot_general x6 -> x8, matrix products: 73.6 us -> 73.2 us  [the longest x2 29.5 us: device_fn(): jnp.einsum('bsuc,uhc->bsh', up_act, w[16:24], preferred_element_type=jnp....]
  transfers between devices with their start and end apart: 12 -> 4, of which waited for: 12 -> 4; matrix products, arithmetic and copies ran while one was open for 9% -> 5% of each run, Pallas kernels for 0% -> 0%
where the time goes in v1:
time: 406 us; the launch traced here: 401 us
  matrix products  119 us (29%)
  Pallas kernels  116 us (29%)
  waiting for transfers between devices  89.5 us (22%)
  local copies, waits for them, and re-layouts  38.7 us (10%)
  other arithmetic  22.1 us (5%)
  between operations  14.6 us (4%)
    pallas_call x1, Pallas kernels, gather_weights(): pl.pallas_call(gather_kernel, out_shape=jax.ShapeDtypeStruct((2 * UNITS,...  116 us
    psum x2, waiting for transfers between devices, device_fn(): down_sum = lax.psum(down_part, 'tp')  46.7 us
    sub x2, matrix products, alibi_attention(): attn_probs = jax.nn.softmax(scores, axis=-1).astype(jnp.bfloat16)  46.2 us
    psum x2, waiting for transfers between devices, device_fn(): attn_sum = lax.psum(attn_part, 'tp')  42.8 us
    dot_general x2, matrix products, device_fn(): jnp.einsum('bsuc,uhc->bsh', up_act, w[16:24], preferred_element_type=jnp....  29.5 us
    dot_general x2, matrix products, alibi_attention(): jnp.einsum('bnqk,bknd->bqnd', attn_probs, value_heads, preferred_element_...  25.3 us
    dot_general x2, matrix products, device_fn(): jnp.einsum('bsh,uhc->bsuc', normed, w[0:6], preferred_element_type=jnp.fl...  13.1 us
    slice x1, local copies, waits for them, and re-layouts, device_fn(): w[8:16]  12.5 us
  transfers between devices with their start and end apart: 4, of which 4 were waited for; matrix products, arithmetic and copies ran while one was open for 5% of the time, Pallas kernels for 0%

profile of v1, /device:TPU:1, one launch (start us, length us, event | category | flops | bytes accessed | tf_op | source)
XLA Modules:
  0.0 400.7 jit_solution(12944675244161736991)
XLA Ops:
  8.2 1.1 reshape.570
  9.4 1.0 bitcast_bitcast_fusion
  11.2 116.2 %torus_gather.1 = bf16[48,4,4,4,16,256]{5,4,3,2,1,0:T(8,128)(2,1)} custom-call(bf16[48,16,256]{2,1,0:T(8,128)(2,1)} %bitcast.225), custom_call_target="tpu_custom_call" | custom-call | tf_op jit(solution)/shard_map/torus_gather/pallas_call | solution.py:152
  127.3 3.1 fusion.189
  130.5 6.8 %fusion.190 = (bf16[6,4,4,4,16,256]{5,4,3,2,1,0:T(8,128)(2,1)}, bf16[6,4,4,4,16,256]{5,4,3,2,1,0:T(8,128)(2,1)}) fusion(bf16[48,4,4,4,16,256]{5,4,3,2,1,0:T(8,128)(2,1)} %torus_gather.1), kind=kLoop, calls=%fused_computation.203 | loop fusion | bytes 12582912 | tf_op jit(solution)/shard_map/slice | solution.py:192
  139.6 2.3 broadcast_subtract_fusion
  141.9 4.7 %copy.32 = bf16[6,256,1024]{2,1,0:T(8,128)(2,1)} copy(bf16[6,256,1024]{1,2,0:T(8,128)(2,1)} %bitcast.218) | data formatting | bytes 6291456 | tf_op jit(solution)/shard_map/bsh,uhc->bsuc/dot_general | solution.py:192
  146.6 7.4 %fusion.82 = bf16[1,1024,3,8,64]{1,4,3,2,0:T(8,128)(2,1)} fusion(f32[3,8,64]{2,1,0:T(8,128)S(1)} %get-tuple-element.23, bf16[3,8,64,1024]{3,2,1,0:T(8,128)(2,1)} %bitcast.224, bf16[1,1024,1024]{2,1,0:T(8,128)(2,1)S(1)} %copy-done, f32[1024]{0:T(1024)S(1)} %bitcast.247, f32[1024]{0:T(1024)S(1)} %bitcast.246, f32[1024]{0:T(1024)S(1)} %add_rsqrt_fusion.3, ...), kind=kOutput, calls=%fused_computation.100 | convolution fusion | flops 3230662656 | bytes 8411136 | tf_op jit(solution)/shard_map/bsh,uhc->bsuc/dot_general | solution.py:192
  154.1 23.3 %fusion.191 = (f32[8,1024]{1,0:T(8,128)S(1)}, f32[8,1024,1024]{1,2,0:T(8,128)}) fusion(f32[1024,1024]{0,1:T(8,128)} %broadcast_subtract_fusion, f32[8]{0:T(128)S(1)} %dynamic_slice.3, pred[1024,1024]{0,1:T(8,128)(4,1)S(1)} %fusion.76, bf16[1,1024,3,8,64]{1,4,3,2,0:T(8,128)(2,1)} %fusion.82), kind=kOutput, calls=%fused_computation.204 | convolution fusion | flops 1124074496 | bytes 40927264 | tf_op jit(solution)/shard_map/sub | solution.py:51
  177.4 12.6 %fusion.143 = bf16[8,64,1024]{2,1,0:T(8,128)(2,1)S(1)} fusion(f32[8,1024,1024]{1,2,0:T(8,128)} %get-tuple-element.38, f32[8,1024]{1,0:T(8,128)S(1)} %get-tuple-element.37, bf16[1,1024,3,8,64]{1,4,3,2,0:T(8,128)(2,1)} %fusion.82), kind=kOutput, calls=%fused_computation.134 | convolution fusion | flops 1091043328 | bytes 35684352 | tf_op jit(solution)/shard_map/bnqk,bknd->bqnd/dot_general | solution.py:52
  190.0 2.6 fusion.140
  192.9 12.5 %fusion.188 = (bf16[8,4,4,4,16,256]{5,4,3,2,1,0:T(8,128)(2,1)}, bf16[8,4,4,4,16,256]{5,4,3,2,1,0:T(8,128)(2,1)}, bf16[8,4,4,4,16,256]{5,4,3,2,1,0:T(8,128)(2,1)}, bf16[8,4,4,4,16,256]{5,4,3,2,1,0:T(8,128)(2,1)}) fusion(bf16[48,4,4,4,16,256]{5,4,3,2,1,0:T(8,128)(2,1)} %torus_gather.1), kind=kLoop, calls=%fused_computation.201 | loop fusion | bytes 33554432 | tf_op jit(solution)/shard_map/slice | solution.py:201
  205.4 15.3 %all-reduce.5.cloned.1.call-done = bf16[1,1024,1024]{2,1,0:T(8,128)(2,1)} async-done(((bf16[1,1024,1024]{2,1,0:T(8,128)(2,1)}), bf16[1,1024,1024]{2,1,0:T(8,128)(2,1)}) %all-reduce.5.cloned.1.call-update) | async-done | bytes 2097168 | tf_op jit(solution)/shard_map/psum | solution.py:198
  220.7 2.4 convert_reduce_fusion.2
  223.2 1.3 copy-done.1
  225.2 14.7 %fusion.84 = bf16[1,1024,1024]{2,1,0:T(8,128)(2,1)} fusion(bf16[8,1024,256]{2,1,0:T(8,128)(2,1)} %bitcast.221, f32[8,256]{1,0:T(8,128)S(1)} %reshape.597, bf16[8,1024,256]{2,1,0:T(8,128)(2,1)} %bitcast.222, bf16[1,1024,1024]{2,1,0:T(8,128)(2,1)} %copy-done.1, f32[1024]{0:T(1024)S(1)} %bitcast.245, f32[1024]{0:T(1024)S(1)} %bitcast.244, ...), kind=kOutput, calls=%fused_computation.102 | convolution fusion | flops 8618246144 | bytes 12607488 | tf_op jit(solution)/shard_map/bsuc,uhc->bsh/dot_general | solution.py:203
  240.0 3.3 copy.35
  243.3 24.2 %all-reduce.7.cloned.1.call-done = bf16[1,1024,1024]{2,1,0:T(8,128)(2,1)} async-done(((bf16[1,1024,1024]{2,1,0:T(8,128)(2,1)}), bf16[1,1024,1024]{2,1,0:T(8,128)(2,1)}) %all-reduce.7.cloned.1.call-update) | async-done | bytes 2097168 | tf_op jit(solution)/shard_map/psum | solution.py:204
  267.5 3.2 convert_reduce_fusion.1
  271.4 5.7 %fusion.83 = bf16[1,1024,3,8,64]{1,4,3,2,0:T(8,128)(2,1)} fusion(f32[3,8,64]{2,1,0:T(8,128)S(1)} %get-tuple-element.24, bf16[3,8,64,1024]{3,2,1,0:T(8,128)(2,1)S(1)} %bitcast.223, bf16[1,1024,1024]{2,1,0:T(8,128)(2,1)S(1)} %get-tuple-element.8, f32[1024]{0:T(1024)S(1)} %bitcast.241, f32[1024]{0:T(1024)S(1)} %bitcast.240, f32[1024]{0:T(1024)S(1)} %add_rsqrt_fusion.1, ...), kind=kOutput, calls=%fused_computation.101 | convolution fusion | flops 3230662656 | bytes 8411136 | tf_op jit(solution)/shard_map/bsh,uhc->bsuc/dot_general | solution.py:192
  277.1 22.9 %fusion.196 = (f32[8,1024]{1,0:T(8,128)S(1)}, f32[8,1024,1024]{1,2,0:T(8,128)}) fusion(f32[1024,1024]{0,1:T(8,128)} %broadcast_subtract_fusion, f32[8]{0:T(128)S(1)} %dynamic_slice.3, pred[1024,1024]{0,1:T(8,128)(4,1)S(1)} %copy-done.9, bf16[1,1024,3,8,64]{1,4,3,2,0:T(8,128)(2,1)} %fusion.83), kind=kOutput, calls=%fused_computation.205 | convolution fusion | flops 1124074496 | bytes 40927264 | tf_op jit(solution)/shard_map/sub | solution.py:51
  300.0 12.8 %fusion.142 = bf16[8,64,1024]{2,1,0:T(8,128)(2,1)S(1)} fusion(f32[8,1024,1024]{1,2,0:T(8,128)} %get-tuple-element.40, f32[8,1024]{1,0:T(8,128)S(1)} %get-tuple-element.39, bf16[1,1024,3,8,64]{1,4,3,2,0:T(8,128)(2,1)} %fusion.83), kind=kOutput, calls=%fused_computation.133 | convolution fusion | flops 1091043328 | bytes 35684352 | tf_op jit(solution)/shard_map/bnqk,bknd->bqnd/dot_general | solution.py:52
  312.8 2.6 fusion.141
  315.5 27.5 %all-reduce.9.cloned.1.call-done = bf16[1,1024,1024]{2,1,0:T(8,128)(2,1)} async-done(((bf16[1,1024,1024]{2,1,0:T(8,128)(2,1)}), bf16[1,1024,1024]{2,1,0:T(8,128)(2,1)}) %all-reduce.9.cloned.1.call-update) | async-done | bytes 2097168 | tf_op jit(solution)/shard_map/psum | solution.py:198
  343.0 2.4 convert_reduce_fusion
  345.5 1.3 copy-done.2
  347.5 14.8 %fusion.85 = bf16[1,1024,1024]{2,1,0:T(8,128)(2,1)} fusion(bf16[8,1024,256]{2,1,0:T(8,128)(2,1)} %bitcast.220, f32[8,256]{1,0:T(8,128)S(1)} %reshape.604, bf16[8,1024,256]{2,1,0:T(8,128)(2,1)} %bitcast.219, bf16[1,1024,1024]{2,1,0:T(8,128)(2,1)} %copy-done.2, f32[1024]{0:T(1024)S(1)} %bitcast.243, f32[1024]{0:T(1024)S(1)} %bitcast.242, ...), kind=kOutput, calls=%fused_computation.103 | convolution fusion | flops 8618246144 | bytes 12607488 | tf_op jit(solution)/shard_map/bsuc,uhc->bsh/dot_general | solution.py:203
  362.5 1.7 copy-done.7
  364.4 1.5 pad_maximum_fusion.1
  365.9 1.5 pad_maximum_fusion
  367.4 22.4 %all-reduce.11.cloned.1.call-done = bf16[1,1024,1024]{2,1,0:T(8,128)(2,1)} async-done(((bf16[1,1024,1024]{2,1,0:T(8,128)(2,1)}), bf16[1,1024,1024]{2,1,0:T(8,128)(2,1)}) %all-reduce.11.cloned.1.call-update) | async-done | bytes 2097168 | tf_op jit(solution)/shard_map/psum | solution.py:204
  389.9 3.9 fusion.71
  (89 shorter events, 7.0 us)
Async XLA Ops:
  7.2 213.6 %all-reduce.5.cloned.1.call-start = ((), (), s32[]{:S(2)}) async-start(), calls=%async_computation | async-start | bytes 4194304 | tf_op jit(solution)/shard_map/psum | solution.py:198
  130.4 6.8 %copy-start.13 = (s32[1,1024]{1,0:T(1,128)S(1)}, s32[1,1024]{1,0:T(1,128)}, u32[]{:S(2)}) copy-start(s32[1,1024]{1,0:T(1,128)} %param.16) | copy-start | bytes 12292
  130.4 7.6 %copy-start = (bf16[1,1024,1024]{2,1,0:T(8,128)(2,1)S(1)}, bf16[1,1024,1024]{2,1,0:T(8,128)(2,1)}, u32[]{:S(2)}) copy-start(bf16[1,1024,1024]{2,1,0:T(8,128)(2,1)} %param.15) | copy-start | bytes 6291460
  137.3 1.8 copy-start.14
  137.3 1.9 copy-start.15
  137.3 1.9 copy-start.20
  139.6 14.5 %copy-start.8 = (pred[1024,1024]{0,1:T(8,128)(4,1)}, pred[1024,1024]{0,1:T(8,128)(4,1)S(1)}, u32[]{:S(2)}) copy-start(pred[1024,1024]{0,1:T(8,128)(4,1)S(1)} %fusion.76) | copy-start | bytes 3145732
  141.9 4.7 %copy-start.21 = (f32[16]{0:T(128)S(1)}, f32[16]{0:T(128)}, u32[]{:S(2)}) copy-start(f32[16]{0:T(128)} %constant.55.clone) | copy-start | bytes 196
  177.4 12.6 %copy-start.11 = (bf16[2,4,4,4,16,256]{5,4,3,2,1,0:T(8,128)(2,1)S(1)}, bf16[2,4,4,4,16,256]{5,4,3,2,1,0:T(8,128)(2,1)}, u32[]{:S(2)}) copy-start(bf16[2,4,4,4,16,256]{5,4,3,2,1,0:T(8,128)(2,1)} %get-tuple-element.16) | copy-start | bytes 3145732
  190.0 2.8 copy-start.12
  190.0 2.8 copy-start.16
  190.0 2.8 copy-start.17
  190.0 2.8 copy-start.18
  192.7 74.8 %all-reduce.7.cloned.1.call-start = ((), (), s32[]{:S(2)}) async-start(), calls=%async_computation.1 | async-start | bytes 4194304 | tf_op jit(solution)/shard_map/psum | solution.py:204
  223.1 1.3 copy-start.1
  225.2 14.8 %copy-start.4 = (bf16[6,4,4,4,16,256]{5,4,3,2,1,0:T(8,128)(2,1)S(1)}, bf16[6,4,4,4,16,256]{5,4,3,2,1,0:T(8,128)(2,1)}, u32[]{:S(2)}) copy-start(bf16[6,4,4,4,16,256]{5,4,3,2,1,0:T(8,128)(2,1)} %get-tuple-element.18) | copy-start | bytes 9437188
  239.9 3.4 copy-start.19
  239.9 103.1 %all-reduce.9.cloned.1.call-start = ((), (), s32[]{:S(2)}) async-start(), calls=%async_computation.2 | async-start | bytes 4194304 | tf_op jit(solution)/shard_map/psum | solution.py:198
  267.5 3.9 copy-start.5
  271.4 5.7 %copy-start.9 = (pred[1024,1024]{0,1:T(8,128)(4,1)S(1)}, pred[1024,1024]{0,1:T(8,128)(4,1)}, u32[]{:S(2)}) copy-start(pred[1024,1024]{0,1:T(8,128)(4,1)} %copy-done.8) | copy-start | bytes 3145732
  300.0 12.8 %copy-start.10 = (bf16[2,4,4,4,16,256]{5,4,3,2,1,0:T(8,128)(2,1)S(1)}, bf16[2,4,4,4,16,256]{5,4,3,2,1,0:T(8,128)(2,1)}, u32[]{:S(2)}) copy-start(bf16[2,4,4,4,16,256]{5,4,3,2,1,0:T(8,128)(2,1)} %get-tuple-element.15) | copy-start | bytes 3145732
  315.4 74.4 %all-reduce.11.cloned.1.call-start = ((), (), s32[]{:S(2)}) async-start(), calls=%async_computation.3 | async-start | bytes 4194304 | tf_op jit(solution)/shard_map/psum | solution.py:204
  345.4 1.3 copy-start.2
  347.5 14.8 %copy-start.6 = (bf16[1,1024,3,8,64]{1,4,3,2,0:T(8,128)(2,1)S(1)}, bf16[1,1024,3,8,64]{1,4,3,2,0:T(8,128)(2,1)}, u32[]{:S(2)}) copy-start(bf16[1,1024,3,8,64]{1,4,3,2,0:T(8,128)(2,1)} %fusion.82) | copy-start | bytes 9437188
  362.3 1.9 copy-start.7
  364.4 25.5 %copy-start.3 = (bf16[1,1024,1024]{2,1,0:T(8,128)(2,1)S(1)}, bf16[1,1024,1024]{2,1,0:T(8,128)(2,1)}, u32[]{:S(2)}) copy-start(bf16[1,1024,1024]{2,1,0:T(8,128)(2,1)} %copy-done.2) | copy-start | bytes 6291460
Sparse Core Ops, SparseCore 0:
  192.8 27.8 all-reduce.4
  240.0 27.4 all-reduce.6
  315.6 27.4 all-reduce.8
  362.4 27.4 all-reduce.10

commit v2 on v1

v2 whole, which is shorter than its diff:
```python
import math
import jax
import jax.numpy as jnp
from jax import lax
from jax.experimental import pallas as pl
from jax.experimental.pallas import tpu as pltpu
from jax.sharding import PartitionSpec as P

LN_EPS = 1e-5
MESH = pl.DeviceIdType.MESH
UNITS = 24
CHUNKS = 16
STAGES = 6
OFFSETS = (0, 1, 4, 5, 8, 10, 12)
HEAD_TICKS = 15
LAYER_TICKS = 14
NT = (((1,), (1,)), ((), ()))
ORDERS = (('x', 'y', 'z'), ('y', 'z', 'x'), ('z', 'x', 'y'))


def alibi_slopes(n_heads):
    closest = 2 ** int(math.floor(math.log2(n_heads)))
    slope_base = 2.0 ** (-8.0 / closest)
    slope_list = [slope_base ** (i + 1) for i in range(closest)]
    extra_base = 2.0 ** (-4.0 / closest)
    slope_list = slope_list + [extra_base ** (2 * i + 1) for i in range(n_heads - closest)]
    return jnp.array(slope_list, dtype=jnp.float32)


class Torus:
    def __init__(self, blocks, send_sem, recv_sem):
        self.blocks, self.send_sem, self.recv_sem = blocks, send_sem, recv_sem
        me = lax.axis_index('wg')
        self.pos = {'z': lax.div(me, 16), 'y': lax.rem(lax.div(me, 4), 4), 'x': lax.rem(me, 4)}
        self.next = {ax: lax.rem(p + 1, 4) for ax, p in self.pos.items()}
        self.prev = {ax: lax.rem(p + 3, 4) for ax, p in self.pos.items()}
        self.right = {ax: self.device({**self.pos, ax: self.next[ax]}) for ax in 'zyx'}
        self.left = {ax: self.device({**self.pos, ax: self.prev[ax]}) for ax in 'zyx'}

    @staticmethod
    def device(pos):
        return pos['z'] * 16 + pos['y'] * 4 + pos['x']

    def view(self, unit, where, cols=None):
        ref = self.blocks.at[unit, where['z'], where['y'], where['x']]
        return ref if cols is None else self.blocks.at[unit, where['z'], where['y'], where['x'], :, cols]

    def barrier(self):
        sem = pltpu.get_barrier_semaphore()
        for ax in 'zyx':
            for dev in (self.left[ax], self.right[ax]):
                pl.semaphore_signal(sem, inc=1, device_id={'wg': dev}, device_id_type=MESH)
        pl.semaphore_signal(sem, inc=1, device_id={'tp': 1 - lax.axis_index('tp')}, device_id_type=MESH)
        pl.semaphore_wait(sem, 7)

    def sends(self, chunk, stage):
        every, low, high = slice(None), slice(0, 2), slice(2, 4)
        out = []
        for color, (a, b, c) in enumerate(ORDERS):
            unit = 3 * chunk + color
            if stage == 0:
                here = dict(self.pos)
                out += [(self.view(unit, here), self.right[a]), (self.view(unit, here), self.left[a])]
            elif stage == 1:
                out += [(self.view(unit, {**self.pos, a: self.prev[a]}, slice(0, 128)), self.right[a]),
                        (self.view(unit, {**self.pos, a: self.next[a]}, slice(128, 256)), self.left[a])]
            elif stage == 2:
                row = {**self.pos, a: every}
                out += [(self.view(unit, row), self.right[b]), (self.view(unit, row), self.left[b])]
            elif stage == 3:
                out += [(self.view(unit, {a: low, b: self.prev[b], c: self.pos[c]}), self.right[b]),
                        (self.view(unit, {a: high, b: self.next[b], c: self.pos[c]}), self.left[b])]
            elif stage == 4:
                plane = {a: every, b: every, c: self.pos[c]}
                out += [(self.view(unit, plane), self.right[c]), (self.view(unit, plane), self.left[c])]
            else:
                slow, fast = (a, b) if 'zyx'.index(a) < 'zyx'.index(b) else (b, a)
                out += [(self.view(unit, {slow: low, fast: every, c: self.prev[c]}), self.right[c]),
                        (self.view(unit, {slow: high, fast: every, c: self.next[c]}), self.left[c])]
        return out

    def start(self, chunk, stage):
        for ref, dev in self.sends(chunk, stage):
            pltpu.make_async_remote_copy(
                src_ref=ref, dst_ref=ref, send_sem=self.send_sem.at[chunk, stage], recv_sem=self.recv_sem.at[chunk, stage],
                device_id={'wg': dev}, device_id_type=MESH).start()

    def wait(self, sem, chunk, stage):
        w = self.blocks
        size = (w.at[0:3, 0, 0, 0:2], w.at[0:3, 0, 0, 0], w.at[0:3, 0, 0:2], w.at[0:3, 0, 0], w.at[0:3, 0:2], w.at[0:3, 0])[stage]
        pltpu.make_async_copy(size, size, sem.at[chunk, stage]).wait()

    def step(self, chunk, stage):
        if stage > 0:
            self.wait(self.recv_sem, chunk, stage - 1)
        if stage < STAGES:
            self.start(chunk, stage)

    def tick(self, t, odd):
        for stage in ((1, 3) if odd else (4, 5, 2, 0, 6)):
            chunk = lax.div(t - OFFSETS[stage], 2)

            @pl.when((t >= OFFSETS[stage]) & (chunk < CHUNKS))
            def _():
                self.step(chunk, stage)


def normalize(values, scale, shift):
    mean = jnp.mean(values, axis=1, keepdims=True)
    centered = values - mean
    variance = jnp.mean(centered * centered, axis=1, keepdims=True)
    return (centered * lax.rsqrt(variance + LN_EPS) * scale + shift).astype(jnp.bfloat16)


def rows(r, size=256):
    return pl.ds(pl.multiple_of(r * size, size), size)


def layers_kernel(x_hbm, mask_ref, slope_ref, ln1s_ref, ln1b_ref, ln2s_ref, ln2b_ref, bqkv_ref, bout_ref, bup_ref, bdown_ref,
                  local_ref, out_hbm, cache_hbm,
                  blocks, x, a, qkv, ctx, act, acc, part, other, bias_cols, limits,
                  send_sem, recv_sem, part_send, part_recv, own_sem, x_sem, cache_sem, out_sem):
    f32, bf16 = jnp.float32, jnp.bfloat16
    torus = Torus(blocks, send_sem, recv_sem)
    partner = {'tp': 1 - lax.axis_index('tp')}
    own = pltpu.make_async_copy(local_ref, blocks.at[:, torus.pos['z'], torus.pos['y'], torus.pos['x']], own_sem)
    own.start()
    x_in = pltpu.make_async_copy(x_hbm, x, x_sem)
    x_in.start()
    torus.barrier()
    own.wait()
    torus.tick(jnp.int32(0), False)

    def row_of(ref, layer):
        both = ref[...].astype(f32)
        return jnp.where(layer == 0, both[0:1], both[1:2])

    def weight(unit):
        return blocks[unit].reshape(1024, 256)

    real = jnp.sum(mask_ref[...].astype(f32), axis=1, keepdims=True)
    key = lax.broadcasted_iota(jnp.int32, (1024, 128), 0).astype(f32)
    lane = lax.broadcasted_iota(jnp.int32, (1024, 128), 1)
    place = key - (1024.0 - real)
    slope = jnp.where(lax.axis_index('tp') == 0, slope_ref[0:1], slope_ref[1:2])
    key_bias = jnp.where(place >= 0.0, place * slope, -1e30)
    first = key_bias.astype(bf16)
    rest = key_bias - first.astype(f32)
    second = rest.astype(bf16)
    third = (rest - second.astype(f32)).astype(bf16)
    which = lax.rem(lane, 3)
    split = jnp.where(which == 0, first.astype(f32), jnp.where(which == 1, second.astype(f32), third.astype(f32)))
    bias_cols[...] = jnp.where(lane < 24, split, 0.0).astype(bf16)
    row = lax.broadcasted_iota(jnp.int32, (256, 256), 0)
    col = lax.broadcasted_iota(jnp.int32, (256, 256), 1)
    limits[0] = jnp.where(col <= row, 3e38, -1e30)
    limits[1] = jnp.where(col == row, -1e29, -3e38)

    x_in.wait()

    def first_norm(r, carry):
        a[rows(r)] = normalize(x[rows(r)].astype(f32), ln1s_ref[0:1].astype(f32), ln1b_ref[0:1].astype(f32))
        return carry

    lax.fori_loop(0, 4, first_norm, 0)

    def head_tick(i, carry):
        torus.tick(2 * i + 1, True)
        torus.tick(2 * i + 2, False)
        return carry

    lax.fori_loop(0, (HEAD_TICKS - 1) // 2, head_tick, 0)

    def exchange(layer, kind, r):
        view = lambda ref: ref.at[kind, rows(r)]
        return pltpu.make_async_remote_copy(
            src_ref=view(part), dst_ref=view(other), send_sem=part_send.at[layer, kind, r], recv_sem=part_recv.at[layer, kind, r],
            device_id=partner, device_id_type=MESH)

    def residual(layer, kind, r, bias):
        exchange(layer, kind, r).wait_recv()
        branch = part[kind, rows(r)].astype(f32) + other[kind, rows(r)].astype(f32)
        total = (x[rows(r)].astype(f32) + branch + bias).astype(bf16)
        x[rows(r)] = total
        return total.astype(f32)

    def attention(pair, carry):
        unit, lanes = lax.div(pair, 2), pl.ds(pl.multiple_of(lax.rem(pair, 2) * 128, 128), 128)
        lane = lax.broadcasted_iota(jnp.int32, (256, 128), 1)
        for r in range(4):
            n = (r + 1) * 256
            q = qkv[unit, r * 256:n, lanes]
            k = jnp.concatenate([qkv[2 + unit, 0:n, lanes], bias_cols[0:n]], axis=1)
            v = jnp.concatenate([qkv[4 + unit, 0:n, lanes], jnp.ones((n, 128), bf16)], axis=1)
            outs = []
            for half in range(2):
                mine = (lane < 64) if half == 0 else (lane >= 64)
                head = 2 * pair + half
                pick = ((lane >= 3 * head) & (lane < 3 * head + 3)).astype(bf16)
                query = jnp.concatenate([jnp.where(mine, q, jnp.zeros_like(q)), pick], axis=1)
                scores = lax.dot_general(query, k, NT, preferred_element_type=f32)
                last = jnp.maximum(jnp.minimum(scores[:, r * 256:], limits[0]), limits[1])
                scores = jnp.concatenate([scores[:, :r * 256], last], axis=1) if r else last
                probs = jnp.exp(scores - jnp.max(scores, axis=1, keepdims=True)).astype(bf16)
                out = jnp.dot(probs, v, preferred_element_type=f32)
                outs.append(out[:, :128] / out[:, 128:])
            ctx[unit, r * 256:n, lanes] = jnp.where(lane < 64, outs[0], outs[1]).astype(bf16)
        return carry

    def layer_body(layer, carry):
        base = layer * UNITS
        t0 = HEAD_TICKS + layer * LAYER_TICKS

        def qkv_unit(j, carry):
            scale = jnp.where(j < 2, 0.125, 1.0)
            cols = pl.ds(pl.multiple_of(j * 256, 256), 256)
            both = bqkv_ref[:, cols].astype(f32)
            bias = jnp.where(layer == 0, both[0:1], both[1:2])
            out = jnp.dot(a[...], weight(base + j), preferred_element_type=f32) + bias
            qkv[j] = (out * scale).astype(bf16)
            return carry

        lax.fori_loop(0, 3, qkv_unit, 0)
        torus.tick(t0, True)
        torus.tick(t0 + 1, False)
        lax.fori_loop(3, 6, qkv_unit, 0)
        cache = pltpu.make_async_copy(qkv.at[2:6], cache_hbm.at[layer], cache_sem)
        cache.start()

        def attend_pair(pair, carry):
            t = t0 + 2 + pair

            @pl.when(lax.rem(pair, 2) == 0)
            def _():
                torus.tick(t, True)

            @pl.when(lax.rem(pair, 2) == 1)
            def _():
                torus.tick(t, False)

            return attention(pair, carry)

        lax.fori_loop(0, 4, attend_pair, 0)

        def send_after(kind, r):
            @pl.when(r > 0)
            def _():
                exchange(layer, kind, r - 1).start()

        def project(r, carry):
            c = jnp.concatenate([ctx[0, rows(r)], ctx[1, rows(r)]], axis=1)
            w = jnp.concatenate([weight(base + 6), weight(base + 7)], axis=1)
            part[0, rows(r)] = lax.dot_general(c, w, NT, preferred_element_type=f32).astype(bf16)
            send_after(0, r)
            return carry

        lax.fori_loop(0, 4, project, 0)
        torus.tick(t0 + 6, True)
        exchange(layer, 0, 3).start()

        def second_norm(r, carry):
            total = residual(layer, 0, r, row_of(bout_ref, layer))
            a[rows(r)] = normalize(total, row_of(ln2s_ref, layer), row_of(ln2b_ref, layer))
            return carry

        lax.fori_loop(0, 4, second_norm, 0)
        torus.tick(t0 + 7, False)

        def up_unit(j, carry):
            cols = pl.ds(pl.multiple_of(j * 256, 256), 256)
            both = bup_ref[:, cols].astype(f32)
            bias = jnp.where(layer == 0, both[0:1], both[1:2])
            out = jnp.dot(a[...], weight(base + 8 + j), preferred_element_type=f32) + bias
            act[j] = jax.nn.gelu(out, approximate=True).astype(bf16)
            return carry

        lax.fori_loop(0, 4, up_unit, 0)
        torus.tick(t0 + 8, True)
        torus.tick(t0 + 9, False)
        lax.fori_loop(4, 8, up_unit, 0)

        def down_product(r, units):
            h = jnp.concatenate([act[j, rows(r)] for j in units], axis=1)
            w = jnp.concatenate([weight(base + 16 + j) for j in units], axis=1)
            return lax.dot_general(h, w, NT, preferred_element_type=f32)

        def down_first(r, carry):
            acc[rows(r)] = down_product(r, (0, 1))
            return carry

        def down_next(r, carry):
            acc[rows(r)] += down_product(r, (2, 3, 4))
            return carry

        def down_last(r, carry):
            part[1, rows(r)] = (acc[rows(r)] + down_product(r, (5, 6, 7))).astype(bf16)
            send_after(1, r)
            return carry

        lax.fori_loop(0, 4, down_first, 0)
        torus.tick(t0 + 10, True)
        torus.tick(t0 + 11, False)
        lax.fori_loop(0, 4, down_next, 0)
        torus.tick(t0 + 12, True)
        torus.tick(t0 + 13, False)
        lax.fori_loop(0, 4, down_last, 0)
        cache.wait()
        exchange(layer, 1, 3).start()

        def finish(r, carry):
            total = residual(layer, 1, r, row_of(bdown_ref, layer))

            @pl.when(layer == 0)
            def _():
                a[rows(r)] = normalize(total, ln1s_ref[1:2].astype(f32), ln1b_ref[1:2].astype(f32))
            return carry

        lax.fori_loop(0, 4, finish, 0)

        def sent(r, carry):
            exchange(layer, 0, r).wait_send()
            exchange(layer, 1, r).wait_send()
            return carry

        lax.fori_loop(0, 4, sent, 0)
        return carry

    lax.fori_loop(0, 2, layer_body, 0)
    out = pltpu.make_async_copy(x, out_hbm, out_sem)
    out.start()

    def drain(chunk, carry):
        for stage in range(STAGES):
            torus.wait(send_sem, chunk, stage)
        return carry

    lax.fori_loop(0, CHUNKS, drain, 0)
    out.wait()


def run_layers(*operands):
    vmem, hbm = pl.BlockSpec(memory_space=pltpu.VMEM), pl.BlockSpec(memory_space=pl.ANY)
    bf16, dma = jnp.bfloat16, pltpu.SemaphoreType.DMA
    return pl.pallas_call(
        layers_kernel,
        out_shape=(jax.ShapeDtypeStruct((1024, 1024), bf16), jax.ShapeDtypeStruct((2, 4, 1024, 256), bf16)),
        in_specs=[hbm] + [vmem] * 10 + [hbm],
        out_specs=(hbm, hbm),
        scratch_shapes=[
            pltpu.VMEM((2 * UNITS, 4, 4, 4, 16, 256), bf16),
            pltpu.VMEM((1024, 1024), bf16),
            pltpu.VMEM((1024, 1024), bf16),
            pltpu.VMEM((6, 1024, 256), bf16),
            pltpu.VMEM((2, 1024, 256), bf16),
            pltpu.VMEM((8, 1024, 256), bf16),
            pltpu.VMEM((1024, 1024), jnp.float32),
            pltpu.VMEM((2, 1024, 1024), bf16),
            pltpu.VMEM((2, 1024, 1024), bf16),
            pltpu.VMEM((1024, 128), bf16),
            pltpu.VMEM((2, 256, 256), jnp.float32),
            dma((CHUNKS, STAGES)),
            dma((CHUNKS, STAGES)),
            dma((2, 2, 4)),
            dma((2, 2, 4)),
            dma,
            dma,
            dma,
            dma,
        ],
        compiler_params=pltpu.CompilerParams(collective_id=0, has_side_effects=True, vmem_limit_bytes=67043328),
        name='two_layers',
    )(*operands)


def pack_local(w_qkv, w_out, w_up, w_down):
    def units(w):
        return w.reshape(w.shape[0], 16, -1, 256).transpose(0, 2, 1, 3)
    qkv = units(w_qkv.transpose(0, 1, 3, 2, 4))
    out = units(w_out.reshape(w_out.shape[0], -1, 16).transpose(0, 2, 1))
    up = units(w_up)
    down = units(w_down.transpose(0, 2, 1))
    return jnp.concatenate([qkv, out, up, down], axis=1).reshape(-1, 16, 256)


def solution(mesh):
    tp_size = mesh.shape['tp']
    batch_axes = ('dp', 'wg')

    def device_fn(hidden, attn_mask, ln1_scale, ln1_bias, w_qkv, b_qkv, w_out, b_out,
                  ln2_scale, ln2_bias, w_up, b_up, w_down, b_down):
        n_layers, _, local_heads, _, head_dim = w_qkv.shape
        slopes = jnp.repeat(alibi_slopes(local_heads * tp_size).reshape(tp_size, local_heads), 3, axis=1)
        slopes = jnp.pad(slopes, ((0, 0), (0, 128 - slopes.shape[1])))
        out, cache = run_layers(
            hidden.reshape(hidden.shape[1:]), attn_mask, slopes, ln1_scale, ln1_bias, ln2_scale, ln2_bias,
            b_qkv.transpose(0, 2, 1, 3).reshape(n_layers, -1), b_out, b_up, b_down,
            pack_local(w_qkv, w_out, w_up, w_down))
        cache = cache.reshape(n_layers, 2, 2, 1024, 256).transpose(1, 0, 3, 2, 4)
        cache = cache.reshape(2, n_layers, 1, 1024, local_heads, head_dim)
        return out.reshape(hidden.shape), cache[0], cache[1]

    replicated = P(None, None)
    in_specs = (P(batch_axes, None, None), P(batch_axes, None), replicated, replicated,
                P(None, 'wg', 'tp', None, None), P(None, 'tp', None, None), P(None, 'tp', None, 'wg'), replicated,
                replicated, replicated, P(None, 'wg', 'tp'), P(None, 'tp'), P(None, 'tp', 'wg'), replicated)
    cache_spec = P(None, batch_axes, None, 'tp', None)
    out_specs = (P(batch_axes, None, None), cache_spec, cache_spec)
    return jax.shard_map(device_fn, mesh=mesh, in_specs=in_specs, out_specs=out_specs, check_vma=False)
```

time: 406 us -> 191 us (0.47); the launches traced: 401 us -> 190 us
  matrix products: 119 us -> 0 us
  waiting for transfers between devices: 89.5 us -> 0 us
  Pallas kernels: 116 us -> 170 us
  other arithmetic: 22.1 us -> 0.79 us
  local copies, waits for them, and re-layouts: 38.7 us -> 19.1 us
  between operations: 14.6 us -> 0.67 us
    psum x4 -> x0, waiting for transfers between devices: 89.5 us -> none  [the longest x2 46.7 us: device_fn(): down_sum = lax.psum(down_part, 'tp')]
    dot_general x8 -> x0, matrix products: 73.2 us -> none  [the longest x2 29.5 us: device_fn(): jnp.einsum('bsuc,uhc->bsh', up_act, w[16:24], preferred_element_type=jnp....]
    pallas_call x1, Pallas kernels: 116 us -> 170 us  [run_layers(): pl.pallas_call(layers_kernel, out_shape=(jax.ShapeDtypeStruct((1024, 1024...]
    sub x2 -> x0, matrix products: 46.2 us -> none  [alibi_attention(): attn_probs = jax.nn.softmax(scores, axis=-1).astype(jnp.bfloat16)]
    slice x4 -> x3, local copies, waits for them, and re-layouts: 22.7 us -> 10.1 us  [device_fn(): return (out.reshape(hidden.shape), cache[0], cache[1])]
    reduce_sum x8 -> x0, other arithmetic: 11.1 us -> none  [the longest x4 8.35 us: layer_norm(): mean_val = jnp.mean(as_float, axis=-1, keepdims=True)]
    dot_general x2 -> x0, local copies, waits for them, and re-layouts: 7.97 us -> none  [device_fn(): jnp.einsum('bsh,uhc->bsuc', normed, w[0:6], preferred_element_type=jnp.fl...]
  transfers between devices with their start and end apart: 4 -> 0, of which waited for: 4 -> 0; matrix products, arithmetic and copies ran while one was open for 5% -> 0% of each run, Pallas kernels for 0% -> 0%
where the time goes in v2:
time: 191 us; the launch traced here: 190 us
  Pallas kernels  170 us (89%)
  local copies, waits for them, and re-layouts  19.1 us (10%)
    pallas_call x1, Pallas kernels, run_layers(): pl.pallas_call(layers_kernel, out_shape=(jax.ShapeDtypeStruct((1024, 1024...  170 us
    slice x3, local copies, waits for them, and re-layouts, device_fn(): return (out.reshape(hidden.shape), cache[0], cache[1])  10.1 us
    unnamed x2, local copies, waits for them, and re-layouts  3.94 us

profile of v2, /device:TPU:1, one launch (start us, length us, event | category | flops | bytes accessed | tf_op | source)
XLA Modules:
  0.0 190.1 jit_solution(12559508135081215763)
XLA Ops:
  0.6 1.4 reshape.50.bqkv_ref
  2.0 0.7 broadcast_in_dim.3
  2.8 0.1 reshape.49
  2.8 0.6 pad.4.slope_ref
  3.4 0.9 copy.23
  4.3 0.1 reshape.52
  4.4 1.1 reshape.51
  5.6 1.0 bitcast_bitcast_fusion
  6.6 0.8 pad_maximum_fusion
  7.4 169.6 %two_layers.1 = (bf16[1024,1024]{1,0:T(8,128)(2,1)}, bf16[2,4,1024,256]{3,2,1,0:T(8,128)(2,1)}) custom-call(bf16[1024,1024]{1,0:T(8,128)(2,1)} %bitcast.33, s32[1,1024]{1,0:T(1,128)} %mask_ref.1, f32[2,128]{1,0:T(2,128)} %pad.4.slope_ref, bf16[2,1024]{1,0:T(2,128)(2,1)} %ln1s_ref.1, bf16[2,1024]{1,0:T(2,128)(2,1)} %ln1b_ref.1, bf16[2,1024]{1,0:T(2,128)(2,1)} %ln2s_ref.1, ...), custom_call_target="tpu_custom_call" | custom-call | tf_op jit(solution)/shard_map/two_layers/pallas_call | solution.py:344
  177.0 3.8 %fusion = (bf16[1,2,1024,2,256]{4,2,3,0,1:T(8,128)(2,1)}, bf16[1,2,1024,2,256]{4,2,3,0,1:T(8,128)(2,1)S(1)}) fusion(bf16[2,2,1024,2,256]{4,2,3,0,1:T(8,128)(2,1)} %bitcast.32), kind=kLoop, calls=%fused_computation.3 | loop fusion | bytes 8388608 | tf_op jit(solution)/shard_map/slice | solution.py:400
  180.8 3.9 %copy.29 = bf16[1,2,1024,2,256]{2,4,3,1,0:T(8,128)(2,1)} copy(bf16[1,2,1024,2,256]{4,2,3,0,1:T(8,128)(2,1)} %get-tuple-element.7) | data formatting | bytes 4194304 | tf_op jit(solution)/shard_map/slice | solution.py:400
  184.7 2.4 %copy.28 = bf16[1,2,1024,2,256]{2,4,3,1,0:T(8,128)(2,1)} copy(bf16[1,2,1024,2,256]{4,2,3,0,1:T(8,128)(2,1)S(1)} %get-tuple-element.8) | data formatting | bytes 4194304 | tf_op jit(solution)/shard_map/slice | solution.py:400
  187.1 3.1 %copy.35 = bf16[1,1024,1024]{2,1,0:T(8,128)(2,1)} copy(bf16[1,1024,1024]{2,1,0:T(8,128)(2,1)} %bitcast.36) | data formatting | bytes 4194304
  (3 shorter events, 0.0 us)

commit v3 on v2

--- a/solution.py
+++ b/solution.py
@@ -1,6 +1,7 @@
 import math
 import jax
 import jax.numpy as jnp
+import numpy as np
 from jax import lax
 from jax.experimental import pallas as pl
 from jax.experimental.pallas import tpu as pltpu
@@ -11,9 +12,19 @@
 UNITS = 24
 CHUNKS = 16
 STAGES = 6
-OFFSETS = (0, 1, 4, 5, 8, 10, 12)
-HEAD_TICKS = 15
-LAYER_TICKS = 14
+SCHEDULE = {
+    'head': ((0, 0, ((0, 0), (1, 0), (2, 0), (3, 0), (4, 0), (5, 0), (6, 0), (7, 0), (8, 0), (9, 0), (10, 0), (11, 0), (12, 0), (13, 0), (14, 0), (15, 0))),),
+    'norm': ((0, 1, ((0, 1),)), (0, 2, ((1, 1), (2, 1), (3, 1), (4, 1), (5, 1))), (0, 3, ((6, 1), (7, 1), (8, 1), (9, 1)))),
+    'qkv': ((0, 0, ((0, 2), (1, 2), (2, 2), (3, 2), (4, 2), (0, 3), (5, 2), (1, 3), (2, 3), (3, 3), (4, 3), (0, 4), (5, 3), (1, 4), (0, 5), (2, 4), (1, 5), (0, 6))), (0, 1, ((3, 4),)), (0, 3, ((4, 4), (1, 6))), (0, 5, ((2, 5),)), (1, 0, ((10, 4), (8, 6))), (1, 3, ((11, 4), (9, 6))), (1, 5, ((12, 3),))),
+    'attn': ((0, 0, ((5, 4),)), (0, 1, ((3, 5),)), (0, 2, ((4, 5), (6, 2), (7, 2))), (0, 3, ((5, 5), (8, 2), (9, 2))), (1, 0, ((13, 3), (14, 3), (15, 3))), (1, 1, ((10, 5),)), (1, 2, ((11, 5), (12, 4))), (1, 3, ((13, 4),))),
+    'proj': ((0, 0, ((2, 6), (6, 3), (10, 1), (11, 1))), (0, 1, ((7, 3), (12, 1), (13, 1), (14, 1))), (0, 2, ((15, 1),)), (1, 0, ((10, 6),)), (1, 1, ((14, 4),))),
+    'mid': ((0, 1, ((6, 4),)), (0, 3, ((7, 4),)), (1, 1, ((12, 5),)), (1, 3, ((13, 5),))),
+    'up': ((0, 1, ((3, 6),)), (0, 2, ((8, 3),)), (0, 3, ((9, 3), (10, 2))), (0, 4, ((4, 6), (6, 5))), (0, 5, ((11, 2),)), (0, 6, ((7, 5),)), (0, 7, ((5, 6), (8, 4))), (1, 0, ((15, 4),)), (1, 1, ((11, 6),)), (1, 3, ((14, 5),)), (1, 4, ((12, 6),)), (1, 7, ((13, 6),))),
+    'd1': ((0, 0, ((6, 6), (9, 4))), (1, 0, ((14, 6),))),
+    'd2': ((0, 0, ((7, 6),)), (0, 1, ((10, 3), (11, 3), (12, 2))), (0, 2, ((8, 5),)), (1, 0, ((15, 6),))),
+    'fin': ((0, 0, ((13, 2), (14, 2), (15, 2))), (0, 1, ((9, 5),))),
+    'd0': ((1, 0, ((15, 5),)),),
+}
 NT = (((1,), (1,)), ((), ()))
 ORDERS = (('x', 'y', 'z'), ('y', 'z', 'x'), ('z', 'x', 'y'))
 
@@ -24,7 +35,7 @@
     slope_list = [slope_base ** (i + 1) for i in range(closest)]
     extra_base = 2.0 ** (-4.0 / closest)
     slope_list = slope_list + [extra_base ** (2 * i + 1) for i in range(n_heads - closest)]
-    return jnp.array(slope_list, dtype=jnp.float32)
+    return np.array(slope_list, dtype=np.float32)
 
 
 class Torus:
@@ -96,13 +107,12 @@
         if stage < STAGES:
             self.start(chunk, stage)
 
-    def tick(self, t, odd):
-        for stage in ((1, 3) if odd else (4, 5, 2, 0, 6)):
-            chunk = lax.div(t - OFFSETS[stage], 2)
-
-            @pl.when((t >= OFFSETS[stage]) & (chunk < CHUNKS))
+    def poll(self, piece, layer, index):
+        for at_layer, at_index, due in SCHEDULE.get(piece, ()):
+            @pl.when((layer == at_layer) & (index == at_index))
             def _():
-                self.step(chunk, stage)
+                for chunk, stage in due:
+                    self.step(chunk, stage)
 
 
 def normalize(values, scale, shift):
@@ -117,19 +127,31 @@
 
 
 def layers_kernel(x_hbm, mask_ref, slope_ref, ln1s_ref, ln1b_ref, ln2s_ref, ln2b_ref, bqkv_ref, bout_ref, bup_ref, bdown_ref,
-                  local_ref, out_hbm, cache_hbm,
-                  blocks, x, a, qkv, ctx, act, acc, part, other, bias_cols, limits,
+                  wout_ref, wqkv_hbm, wup_hbm, wdown_hbm, out_hbm, cache_hbm,
+                  blocks, x, a, qkv, ctx, act, acc, part, other, bias_cols, limits, bias_rows,
                   send_sem, recv_sem, part_send, part_recv, own_sem, x_sem, cache_sem, out_sem):
     f32, bf16 = jnp.float32, jnp.bfloat16
     torus = Torus(blocks, send_sem, recv_sem)
     partner = {'tp': 1 - lax.axis_index('tp')}
-    own = pltpu.make_async_copy(local_ref, blocks.at[:, torus.pos['z'], torus.pos['y'], torus.pos['x']], own_sem)
-    own.start()
+    mine = (torus.pos['z'], torus.pos['y'], torus.pos['x'])
+    own = []
+    for layer in range(2):
+        for first, weights, count in ((0, wqkv_hbm, 6), (8, wup_hbm, 8), (16, wdown_hbm, 8)):
+            own += [pltpu.make_async_copy(weights.at[layer, :, j * 256:(j + 1) * 256],
+                                          blocks.at[(layer * UNITS + first + j,) + mine], own_sem) for j in range(count)]
+    for copy in own:
+        copy.start()
     x_in = pltpu.make_async_copy(x_hbm, x, x_sem)
     x_in.start()
+    for layer in range(2):
+        flat = jnp.concatenate([wout_ref[layer, head] for head in range(8)], axis=1)
+        for j in range(2):
+            blocks[(layer * UNITS + 6 + j,) + mine] = flat[:, j * 256:(j + 1) * 256]
     torus.barrier()
-    own.wait()
-    torus.tick(jnp.int32(0), False)
+    whole = blocks.at[0:44, 0, 0, 0]
+    pltpu.make_async_copy(whole, whole, own_sem).wait()
+    zero = jnp.int32(0)
+    torus.poll('head', zero, zero)
 
     def row_of(ref, layer):
         both = ref[...].astype(f32)
@@ -156,20 +178,20 @@
     limits[0] = jnp.where(col <= row, 3e38, -1e30)
     limits[1] = jnp.where(col == row, -1e29, -3e38)
 
+    for layer in range(2):
+        for kind in range(3):
+            heads = bqkv_ref[layer, kind].astype(f32)
+            for j in range(2):
+                bias_rows[layer * 6 + kind * 2 + j] = jnp.concatenate([heads[h:h + 1] for h in range(4 * j, 4 * j + 4)], axis=1)
+
     x_in.wait()
 
     def first_norm(r, carry):
+        torus.poll('norm', zero, r)
         a[rows(r)] = normalize(x[rows(r)].astype(f32), ln1s_ref[0:1].astype(f32), ln1b_ref[0:1].astype(f32))
         return carry
 
     lax.fori_loop(0, 4, first_norm, 0)
-
-    def head_tick(i, carry):
-        torus.tick(2 * i + 1, True)
-        torus.tick(2 * i + 2, False)
-        return carry
-
-    lax.fori_loop(0, (HEAD_TICKS - 1) // 2, head_tick, 0)
 
     def exchange(layer, kind, r):
         view = lambda ref: ref.at[kind, rows(r)]
@@ -209,35 +231,20 @@
 
     def layer_body(layer, carry):
         base = layer * UNITS
-        t0 = HEAD_TICKS + layer * LAYER_TICKS
 
         def qkv_unit(j, carry):
+            torus.poll('qkv', layer, j)
             scale = jnp.where(j < 2, 0.125, 1.0)
-            cols = pl.ds(pl.multiple_of(j * 256, 256), 256)
-            both = bqkv_ref[:, cols].astype(f32)
-            bias = jnp.where(layer == 0, both[0:1], both[1:2])
-            out = jnp.dot(a[...], weight(base + j), preferred_element_type=f32) + bias
+            out = jnp.dot(a[...], weight(base + j), preferred_element_type=f32) + bias_rows[layer * 6 + j]
             qkv[j] = (out * scale).astype(bf16)
             return carry
 
-        lax.fori_loop(0, 3, qkv_unit, 0)
-        torus.tick(t0, True)
-        torus.tick(t0 + 1, False)
-        lax.fori_loop(3, 6, qkv_unit, 0)
+        lax.fori_loop(0, 6, qkv_unit, 0)
         cache = pltpu.make_async_copy(qkv.at[2:6], cache_hbm.at[layer], cache_sem)
         cache.start()
 
         def attend_pair(pair, carry):
-            t = t0 + 2 + pair
-
-            @pl.when(lax.rem(pair, 2) == 0)
-            def _():
-                torus.tick(t, True)
-
-            @pl.when(lax.rem(pair, 2) == 1)
-            def _():
-                torus.tick(t, False)
-
+            torus.poll('attn', layer, pair)
             return attention(pair, carry)
 
         lax.fori_loop(0, 4, attend_pair, 0)
@@ -248,6 +255,7 @@
                 exchange(layer, kind, r - 1).start()
 
         def project(r, carry):
+            torus.poll('proj', layer, r)
             c = jnp.concatenate([ctx[0, rows(r)], ctx[1, rows(r)]], axis=1)
             w = jnp.concatenate([weight(base + 6), weight(base + 7)], axis=1)
             part[0, rows(r)] = lax.dot_general(c, w, NT, preferred_element_type=f32).astype(bf16)
@@ -255,18 +263,18 @@
             return carry
 
         lax.fori_loop(0, 4, project, 0)
-        torus.tick(t0 + 6, True)
         exchange(layer, 0, 3).start()
 
         def second_norm(r, carry):
+            torus.poll('mid', layer, r)
             total = residual(layer, 0, r, row_of(bout_ref, layer))
             a[rows(r)] = normalize(total, row_of(ln2s_ref, layer), row_of(ln2b_ref, layer))
             return carry
 
         lax.fori_loop(0, 4, second_norm, 0)
-        torus.tick(t0 + 7, False)
 
         def up_unit(j, carry):
+            torus.poll('up', layer, j)
             cols = pl.ds(pl.multiple_of(j * 256, 256), 256)
             both = bup_ref[:, cols].astype(f32)
             bias = jnp.where(layer == 0, both[0:1], both[1:2])
@@ -274,10 +282,7 @@
             act[j] = jax.nn.gelu(out, approximate=True).astype(bf16)
             return carry
 
-        lax.fori_loop(0, 4, up_unit, 0)
-        torus.tick(t0 + 8, True)
-        torus.tick(t0 + 9, False)
-        lax.fori_loop(4, 8, up_unit, 0)
+        lax.fori_loop(0, 8, up_unit, 0)
 
         def down_product(r, units):
             h = jnp.concatenate([act[j, rows(r)] for j in units], axis=1)
@@ -285,29 +290,29 @@
             return lax.dot_general(h, w, NT, preferred_element_type=f32)
 
         def down_first(r, carry):
+            torus.poll('d0', layer, r)
             acc[rows(r)] = down_product(r, (0, 1))
             return carry
 
         def down_next(r, carry):
+            torus.poll('d1', layer, r)
             acc[rows(r)] += down_product(r, (2, 3, 4))
             return carry
 
         def down_last(r, carry):
+            torus.poll('d2', layer, r)
             part[1, rows(r)] = (acc[rows(r)] + down_product(r, (5, 6, 7))).astype(bf16)
             send_after(1, r)
             return carry
 
         lax.fori_loop(0, 4, down_first, 0)
-        torus.tick(t0 + 10, True)
-        torus.tick(t0 + 11, False)
         lax.fori_loop(0, 4, down_next, 0)
-        torus.tick(t0 + 12, True)
-        torus.tick(t0 + 13, False)
         lax.fori_loop(0, 4, down_last, 0)
         cache.wait()
         exchange(layer, 1, 3).start()
 
         def finish(r, carry):
+            torus.poll('fin', layer, r)
             total = residual(layer, 1, r, row_of(bdown_ref, layer))
 
             @pl.when(layer == 0)
@@ -344,7 +349,7 @@
     return pl.pallas_call(
         layers_kernel,
         out_shape=(jax.ShapeDtypeStruct((1024, 1024), bf16), jax.ShapeDtypeStruct((2, 4, 1024, 256), bf16)),
-        in_specs=[hbm] + [vmem] * 10 + [hbm],
+        in_specs=[hbm] + [vmem] * 11 + [hbm] * 3,
         out_specs=(hbm, hbm),
         scratch_shapes=[
             pltpu.VMEM((2 * UNITS, 4, 4, 4, 16, 256), bf16),
@@ -358,6 +363,7 @@
             pltpu.VMEM((2, 1024, 1024), bf16),
             pltpu.VMEM((1024, 128), bf16),
             pltpu.VMEM((2, 256, 256), jnp.float32),
+            pltpu.VMEM((12, 1, 256), jnp.float32),
             dma((CHUNKS, STAGES)),
             dma((CHUNKS, STAGES)),
             dma((2, 2, 4)),
@@ -372,14 +378,25 @@
     )(*operands)
 
 
-def pack_local(w_qkv, w_out, w_up, w_down):
-    def units(w):
-        return w.reshape(w.shape[0], 16, -1, 256).transpose(0, 2, 1, 3)
-    qkv = units(w_qkv.transpose(0, 1, 3, 2, 4))
-    out = units(w_out.reshape(w_out.shape[0], -1, 16).transpose(0, 2, 1))
-    up = units(w_up)
-    down = units(w_down.transpose(0, 2, 1))
-    return jnp.concatenate([qkv, out, up, down], axis=1).reshape(-1, 16, 256)
+def finish_kernel(x_ref, key_ref, value_ref, out_ref, key_out, value_out):
+    out_ref[...] = x_ref[...]
+    key_out[0] = key_ref[0, 0].T
+    value_out[0] = value_ref[0, 0].T
+
+
+def finish_outputs(x, cache):
+    bf16 = jnp.bfloat16
+    across = pl.BlockSpec((1, 128, 1024), lambda i: (i // 4, i % 4, 0))
+    return pl.pallas_call(
+        finish_kernel,
+        grid=(8,),
+        out_shape=(jax.ShapeDtypeStruct(x.shape, bf16),) + (jax.ShapeDtypeStruct((2, 512, 1024), bf16),) * 2,
+        in_specs=[pl.BlockSpec((128, 1024), lambda i: (i, 0)),
+                  pl.BlockSpec((1, 1, 1024, 128), lambda i: (i // 4, (i % 4) // 2, 0, i % 2)),
+                  pl.BlockSpec((1, 1, 1024, 128), lambda i: (i // 4, 2 + (i % 4) // 2, 0, i % 2))],
+        out_specs=(pl.BlockSpec((128, 1024), lambda i: (i, 0)), across, across),
+        name='finish_outputs',
+    )(x, cache, cache)
 
 
 def solution(mesh):
@@ -389,15 +406,15 @@
     def device_fn(hidden, attn_mask, ln1_scale, ln1_bias, w_qkv, b_qkv, w_out, b_out,
                   ln2_scale, ln2_bias, w_up, b_up, w_down, b_down):
         n_layers, _, local_heads, _, head_dim = w_qkv.shape
-        slopes = jnp.repeat(alibi_slopes(local_heads * tp_size).reshape(tp_size, local_heads), 3, axis=1)
-        slopes = jnp.pad(slopes, ((0, 0), (0, 128 - slopes.shape[1])))
+        slopes = np.zeros((tp_size, 128), np.float32)
+        slopes[:, :3 * local_heads] = np.repeat(alibi_slopes(local_heads * tp_size).reshape(tp_size, local_heads), 3, axis=1)
         out, cache = run_layers(
             hidden.reshape(hidden.shape[1:]), attn_mask, slopes, ln1_scale, ln1_bias, ln2_scale, ln2_bias,
-            b_qkv.transpose(0, 2, 1, 3).reshape(n_layers, -1), b_out, b_up, b_down,
-            pack_local(w_qkv, w_out, w_up, w_down))
-        cache = cache.reshape(n_layers, 2, 2, 1024, 256).transpose(1, 0, 3, 2, 4)
-        cache = cache.reshape(2, n_layers, 1, 1024, local_heads, head_dim)
-        return out.reshape(hidden.shape), cache[0], cache[1]
+            b_qkv.transpose(0, 2, 1, 3), b_out, b_up, b_down, w_out.transpose(0, 1, 3, 2),
+            w_qkv.transpose(0, 1, 3, 2, 4).reshape(n_layers, 16, -1), w_up, w_down.transpose(0, 2, 1))
+        out, keys, values = finish_outputs(out, cache)
+        caches = [c.reshape(n_layers, 1, local_heads, head_dim, 1024).transpose(0, 1, 4, 2, 3) for c in (keys, values)]
+        return out.reshape(hidden.shape), *caches
 
     replicated = P(None, None)
     in_specs = (P(batch_axes, None, None), P(batch_axes, None), replicated, replicated,

time: 191 us -> 134 us (0.70)
  Pallas kernels: 170 us -> 132 us
  local copies, waits for them, and re-layouts: 19.1 us -> 1.76 us
    pallas_call x1, Pallas kernels: 170 us -> 124 us  [run_layers(): pl.pallas_call(layers_kernel, out_shape=(jax.ShapeDtypeStruct((1024, 1024...]
    slice x3 -> x0, local copies, waits for them, and re-layouts: 10.1 us -> none  [device_fn(): return (out.reshape(hidden.shape), cache[0], cache[1])]
    pallas_call x0 -> x1, Pallas kernels: none -> 7.95 us  [finish_outputs(): pl.pallas_call(finish_kernel, grid=(8,), out_shape=(jax.ShapeDtypeStruct(...]
    unnamed x2 -> x0, local copies, waits for them, and re-layouts: 3.94 us -> none
where the time goes in v3:
time: 134 us
  Pallas kernels  132 us (99%)
  local copies, waits for them, and re-layouts  1.76 us (1%)
    pallas_call x1, Pallas kernels, run_layers(): pl.pallas_call(layers_kernel, out_shape=(jax.ShapeDtypeStruct((1024, 1024...  124 us
    pallas_call x1, Pallas kernels, finish_outputs(): pl.pallas_call(finish_kernel, grid=(8,), out_shape=(jax.ShapeDtypeStruct(...  7.95 us

profile of v3, /device:TPU:1, one launch (start us, length us, event | category | flops | bytes accessed | tf_op | source)
XLA Modules:
  0.0 134.0 jit_solution(4223071441405541453)
XLA Ops:
  0.6 1.8 %reshape.22.wqkv_hbm = bf16[2,16,1536]{2,1,0:T(8,128)(2,1)} reshape(bf16[2,16,3,8,64]{4,3,2,1,0:T(8,128)(2,1)} %bitcast.19) | data formatting | bytes 196608 | tf_op jit(solution)/shard_map/reshape | solution.py:414
  2.4 123.7 %two_layers.1 = (bf16[1024,1024]{1,0:T(8,128)(2,1)}, bf16[2,4,1024,256]{3,2,1,0:T(8,128)(2,1)}) custom-call(bf16[1024,1024]{1,0:T(8,128)(2,1)} %bitcast.18, s32[1,1024]{1,0:T(1,128)} %mask_ref.1, f32[2,128]{1,0:T(2,128)} %constant.2.clone.slope_ref, bf16[2,1024]{1,0:T(2,128)(2,1)} %ln1s_ref.1, bf16[2,1024]{1,0:T(2,128)(2,1)} %ln1b_ref.1, ...), custom_call_target="tpu_custom_call" | custom-call | tf_op jit(solution)/shard_map/two_layers/pallas_call | solution.py:349
  126.1 8.0 %finish_outputs.1 = (bf16[1024,1024]{1,0:T(8,128)(2,1)}, bf16[2,512,1024]{2,1,0:T(8,128)(2,1)}, bf16[2,512,1024]{2,1,0:T(8,128)(2,1)}) custom-call(bf16[1024,1024]{1,0:T(8,128)(2,1)} %get-tuple-element.8.x_ref, bf16[2,4,1024,256]{3,2,1,0:T(8,128)(2,1)} %get-tuple-element.9.key_ref.value_ref, bf16[2,4,1024,256]{3,2,1,0:T(8,128)(2,1)} %get-tuple-element.9.key_ref.value_ref), custom_call_target="tpu_custom_call" | custom-call | tf_op jit(solution)/shard_map/finish_outputs/pallas_call | solution.py:390

commit v4 on v3

--- a/solution.py
+++ b/solution.py
@@ -8,22 +8,25 @@
 from jax.sharding import PartitionSpec as P
 
 LN_EPS = 1e-5
+GELU_A = math.sqrt(2.0 / math.pi)
+GELU_B = 0.044715 * GELU_A
 MESH = pl.DeviceIdType.MESH
 UNITS = 24
-CHUNKS = 16
+HALVES = 4
+CHUNKS = 18
+DIRECT = (0,)
 STAGES = 6
 SCHEDULE = {
-    'head': ((0, 0, ((0, 0), (1, 0), (2, 0), (3, 0), (4, 0), (5, 0), (6, 0), (7, 0), (8, 0), (9, 0), (10, 0), (11, 0), (12, 0), (13, 0), (14, 0), (15, 0))),),
-    'norm': ((0, 1, ((0, 1),)), (0, 2, ((1, 1), (2, 1), (3, 1), (4, 1), (5, 1))), (0, 3, ((6, 1), (7, 1), (8, 1), (9, 1)))),
-    'qkv': ((0, 0, ((0, 2), (1, 2), (2, 2), (3, 2), (4, 2), (0, 3), (5, 2), (1, 3), (2, 3), (3, 3), (4, 3), (0, 4), (5, 3), (1, 4), (0, 5), (2, 4), (1, 5), (0, 6))), (0, 1, ((3, 4),)), (0, 3, ((4, 4), (1, 6))), (0, 5, ((2, 5),)), (1, 0, ((10, 4), (8, 6))), (1, 3, ((11, 4), (9, 6))), (1, 5, ((12, 3),))),
-    'attn': ((0, 0, ((5, 4),)), (0, 1, ((3, 5),)), (0, 2, ((4, 5), (6, 2), (7, 2))), (0, 3, ((5, 5), (8, 2), (9, 2))), (1, 0, ((13, 3), (14, 3), (15, 3))), (1, 1, ((10, 5),)), (1, 2, ((11, 5), (12, 4))), (1, 3, ((13, 4),))),
-    'proj': ((0, 0, ((2, 6), (6, 3), (10, 1), (11, 1))), (0, 1, ((7, 3), (12, 1), (13, 1), (14, 1))), (0, 2, ((15, 1),)), (1, 0, ((10, 6),)), (1, 1, ((14, 4),))),
-    'mid': ((0, 1, ((6, 4),)), (0, 3, ((7, 4),)), (1, 1, ((12, 5),)), (1, 3, ((13, 5),))),
-    'up': ((0, 1, ((3, 6),)), (0, 2, ((8, 3),)), (0, 3, ((9, 3), (10, 2))), (0, 4, ((4, 6), (6, 5))), (0, 5, ((11, 2),)), (0, 6, ((7, 5),)), (0, 7, ((5, 6), (8, 4))), (1, 0, ((15, 4),)), (1, 1, ((11, 6),)), (1, 3, ((14, 5),)), (1, 4, ((12, 6),)), (1, 7, ((13, 6),))),
-    'd1': ((0, 0, ((6, 6), (9, 4))), (1, 0, ((14, 6),))),
-    'd2': ((0, 0, ((7, 6),)), (0, 1, ((10, 3), (11, 3), (12, 2))), (0, 2, ((8, 5),)), (1, 0, ((15, 6),))),
-    'fin': ((0, 0, ((13, 2), (14, 2), (15, 2))), (0, 1, ((9, 5),))),
-    'd0': ((1, 0, ((15, 5),)),),
+    'head': ((0, 0, ((0, 0), (1, 0), (2, 0), (3, 0), (4, 0), (5, 0), (6, 0), (7, 0), (8, 0), (9, 0), (10, 0), (11, 0), (12, 0), (13, 0), (14, 0), (15, 0), (16, 0), (17, 0))),),
+    'qkv': ((0, 0, ((0, 1), (0, 2), (0, 3), (9, 1), (1, 1), (2, 1), (3, 1), (4, 1), (5, 1), (6, 1), (7, 1), (8, 1), (10, 1), (11, 1), (12, 1), (13, 1), (14, 1), (15, 1), (16, 1), (9, 2), (1, 2), (2, 2), (7, 2), (0, 4), (9, 3), (3, 2), (4, 2), (2, 3), (7, 3), (1, 3), (5, 2), (0, 5), (6, 2), (3, 3), (4, 3), (8, 2), (7, 4), (0, 6), (1, 4))), (0, 1, ((1, 5), (2, 5), (4, 4), (1, 6), (5, 4))), (0, 2, ((2, 6), (4, 5))), (0, 3, ((3, 6),)), (1, 0, ((10, 6), (11, 5))), (1, 2, ((11, 6), (13, 5)))),
+    'attn': ((0, 0, ((2, 4), (5, 3), (6, 3), (3, 4))), (0, 1, ((3, 5), (6, 4))), (0, 2, ((7, 5), (8, 3), (9, 4))), (0, 3, ((5, 5), (10, 2), (6, 5))), (1, 0, ((14, 4),)), (1, 1, ((12, 5), (15, 4))), (1, 2, ((16, 4),)), (1, 3, ((14, 5), (17, 3)))),
+    'proj': ((0, 0, ((4, 6),)), (0, 2, ((8, 4),)), (1, 0, ((12, 6), (15, 5)))),
+    'mid': ((0, 1, ((9, 5),)), (0, 3, ((11, 2),)), (1, 1, ((16, 5),))),
+    'up': ((0, 0, ((10, 3), (12, 2))), (0, 1, ((5, 6), (13, 2))), (0, 2, ((14, 2), (15, 2))), (0, 3, ((16, 2),)), (0, 4, ((6, 6), (8, 5))), (0, 5, ((17, 1),)), (0, 6, ((11, 3),)), (0, 7, ((7, 6), (10, 4))), (1, 0, ((17, 4),)), (1, 1, ((13, 6),)), (1, 4, ((14, 6),)), (1, 7, ((15, 6),))),
+    'd0': ((0, 2, ((12, 3), (13, 3))), (0, 3, ((14, 3),)), (1, 0, ((17, 5),))),
+    'd1': ((0, 0, ((8, 6), (15, 3), (16, 3))), (0, 2, ((11, 4),)), (1, 0, ((16, 6),))),
+    'd2': ((0, 0, ((9, 6), (17, 2))), (0, 2, ((10, 5),)), (0, 3, ((12, 4),)), (1, 0, ((17, 6),))),
+    'fin': ((0, 2, ((13, 4),)),),
 }
 NT = (((1,), (1,)), ((), ()))
 ORDERS = (('x', 'y', 'z'), ('y', 'z', 'x'), ('z', 'x', 'y'))
@@ -46,48 +49,58 @@
         self.next = {ax: lax.rem(p + 1, 4) for ax, p in self.pos.items()}
         self.prev = {ax: lax.rem(p + 3, 4) for ax, p in self.pos.items()}
         self.right = {ax: self.device({**self.pos, ax: self.next[ax]}) for ax in 'zyx'}
+        self.across = {ax: self.device({**self.pos, ax: lax.rem(self.pos[ax] + 2, 4)}) for ax in 'zyx'}
         self.left = {ax: self.device({**self.pos, ax: self.prev[ax]}) for ax in 'zyx'}
 
     @staticmethod
     def device(pos):
         return pos['z'] * 16 + pos['y'] * 4 + pos['x']
 
-    def view(self, unit, where, cols=None):
-        ref = self.blocks.at[unit, where['z'], where['y'], where['x']]
-        return ref if cols is None else self.blocks.at[unit, where['z'], where['y'], where['x'], :, cols]
+    def view(self, unit, where, cols=slice(0, 256)):
+        return self.blocks.at[unit, where['z'], where['y'], where['x'], :, cols]
 
     def barrier(self):
         sem = pltpu.get_barrier_semaphore()
         for ax in 'zyx':
-            for dev in (self.left[ax], self.right[ax]):
+            for dev in (self.left[ax], self.right[ax], self.across[ax]):
                 pl.semaphore_signal(sem, inc=1, device_id={'wg': dev}, device_id_type=MESH)
         pl.semaphore_signal(sem, inc=1, device_id={'tp': 1 - lax.axis_index('tp')}, device_id_type=MESH)
-        pl.semaphore_wait(sem, 7)
+        pl.semaphore_wait(sem, 10)
+
+    def part(self, chunk):
+        if chunk < HALVES:
+            return 3 * (chunk // 2), (chunk % 2) * 128, 128
+        return 3 * (chunk - HALVES // 2), 0, 256
 
     def sends(self, chunk, stage):
         every, low, high = slice(None), slice(0, 2), slice(2, 4)
+        first, start, width = self.part(chunk)
+        cols = slice(start, start + width)
         out = []
         for color, (a, b, c) in enumerate(ORDERS):
-            unit = 3 * chunk + color
-            if stage == 0:
-                here = dict(self.pos)
-                out += [(self.view(unit, here), self.right[a]), (self.view(unit, here), self.left[a])]
+            unit = first + color
+            if stage in (0, 2, 4):
+                axis = (a, b, c)[stage // 2]
+                held = {**self.pos, **{ax: every for ax in (a, b)[:stage // 2]}}
+                ref = self.view(unit, held, cols)
+                out += [(ref, self.right[axis]), (ref, self.left[axis])]
+                if chunk in DIRECT and stage < 4:
+                    out.append((ref, self.across[axis]))
             elif stage == 1:
-                out += [(self.view(unit, {**self.pos, a: self.prev[a]}, slice(0, 128)), self.right[a]),
-                        (self.view(unit, {**self.pos, a: self.next[a]}, slice(128, 256)), self.left[a])]
-            elif stage == 2:
-                row = {**self.pos, a: every}
-                out += [(self.view(unit, row), self.right[b]), (self.view(unit, row), self.left[b])]
+                ahead, back = {**self.pos, a: self.prev[a]}, {**self.pos, a: self.next[a]}
+                if width == 256:
+                    out += [(self.view(unit, ahead, slice(0, 128)), self.right[a]), (self.view(unit, back, slice(128, 256)), self.left[a])]
+                elif chunk % 2 == 0:
+                    out.append((self.view(unit, ahead, cols), self.right[a]))
+                else:
+                    out.append((self.view(unit, back, cols), self.left[a]))
             elif stage == 3:
-                out += [(self.view(unit, {a: low, b: self.prev[b], c: self.pos[c]}), self.right[b]),
-                        (self.view(unit, {a: high, b: self.next[b], c: self.pos[c]}), self.left[b])]
-            elif stage == 4:
-                plane = {a: every, b: every, c: self.pos[c]}
-                out += [(self.view(unit, plane), self.right[c]), (self.view(unit, plane), self.left[c])]
+                out += [(self.view(unit, {a: low, b: self.prev[b], c: self.pos[c]}, cols), self.right[b]),
+                        (self.view(unit, {a: high, b: self.next[b], c: self.pos[c]}, cols), self.left[b])]
             else:
                 slow, fast = (a, b) if 'zyx'.index(a) < 'zyx'.index(b) else (b, a)
-                out += [(self.view(unit, {slow: low, fast: every, c: self.prev[c]}), self.right[c]),
-                        (self.view(unit, {slow: high, fast: every, c: self.next[c]}), self.left[c])]
+                out += [(self.view(unit, {slow: low, fast: every, c: self.prev[c]}, cols), self.right[c]),
+                        (self.view(unit, {slow: high, fast: every, c: self.next[c]}, cols), self.left[c])]
         return out
 
     def start(self, chunk, stage):
@@ -97,13 +110,21 @@
                 device_id={'wg': dev}, device_id_type=MESH).start()
 
     def wait(self, sem, chunk, stage):
-        w = self.blocks
-        size = (w.at[0:3, 0, 0, 0:2], w.at[0:3, 0, 0, 0], w.at[0:3, 0, 0:2], w.at[0:3, 0, 0], w.at[0:3, 0:2], w.at[0:3, 0])[stage]
+        every, three = slice(None), slice(0, 3)
+        peers = three if chunk in DIRECT else slice(0, 2)
+        where = ((0, 0, peers), (0, 0, 0), (0, peers, every), (0, 0, every), (slice(0, 2), every, every), (0, every, every))[stage]
+        size = self.blocks.at[(three,) + where + (every, slice(0, self.part(chunk)[2]))]
         pltpu.make_async_copy(size, size, sem.at[chunk, stage]).wait()
 
+    def used(self, chunk, stage):
+        return stage < STAGES and not (chunk in DIRECT and stage in (1, 3))
+
     def step(self, chunk, stage):
-        if stage > 0:
-            self.wait(self.recv_sem, chunk, stage - 1)
+        before = [n for n in range(stage) if self.used(chunk, n)]
+        if stage < STAGES and not self.used(chunk, stage):
+            return
+        if before:
+            self.wait(self.recv_sem, chunk, before[-1])
         if stage < STAGES:
             self.start(chunk, stage)
 
@@ -122,14 +143,19 @@
     return (centered * lax.rsqrt(variance + LN_EPS) * scale + shift).astype(jnp.bfloat16)
 
 
+def gelu(h):
+    half = 0.5 * h
+    return half + half * jnp.tanh(h * (GELU_A + GELU_B * (h * h)))
+
+
 def rows(r, size=256):
     return pl.ds(pl.multiple_of(r * size, size), size)
 
 
 def layers_kernel(x_hbm, mask_ref, slope_ref, ln1s_ref, ln1b_ref, ln2s_ref, ln2b_ref, bqkv_ref, bout_ref, bup_ref, bdown_ref,
-                  wout_ref, wqkv_hbm, wup_hbm, wdown_hbm, out_hbm, cache_hbm,
-                  blocks, x, a, qkv, ctx, act, acc, part, other, bias_cols, limits, bias_rows,
-                  send_sem, recv_sem, part_send, part_recv, own_sem, x_sem, cache_sem, out_sem):
+                  wout_ref, wqkv_hbm, wup_hbm, wdown_hbm, out_hbm, key_hbm, value_hbm,
+                  blocks, x, a, qkv, ctx, act, acc, part, other, bias_cols, limits, bias_rows, keys, values,
+                  send_sem, recv_sem, part_send, part_recv, own_sem, x_sem, key_sem, value_sem, out_sem):
     f32, bf16 = jnp.float32, jnp.bfloat16
     torus = Torus(blocks, send_sem, recv_sem)
     partner = {'tp': 1 - lax.axis_index('tp')}
@@ -137,8 +163,10 @@
     own = []
     for layer in range(2):
         for first, weights, count in ((0, wqkv_hbm, 6), (8, wup_hbm, 8), (16, wdown_hbm, 8)):
-            own += [pltpu.make_async_copy(weights.at[layer, :, j * 256:(j + 1) * 256],
-                                          blocks.at[(layer * UNITS + first + j,) + mine], own_sem) for j in range(count)]
+            for j in range(count):
+                at = (j % 3) * 512 + (j // 3) * 256 if first == 0 else j * 256
+                own.append(pltpu.make_async_copy(weights.at[layer, :, at:at + 256],
+                                                 blocks.at[(layer * UNITS + first + j,) + mine], own_sem))
     for copy in own:
         copy.start()
     x_in = pltpu.make_async_copy(x_hbm, x, x_sem)
@@ -206,7 +234,7 @@
         x[rows(r)] = total
         return total.astype(f32)
 
-    def attention(pair, carry):
+    def attention(layer, pair, carry):
         unit, lanes = lax.div(pair, 2), pl.ds(pl.multiple_of(lax.rem(pair, 2) * 128, 128), 128)
         lane = lax.broadcasted_iota(jnp.int32, (256, 128), 1)
         for r in range(4):
@@ -214,40 +242,65 @@
             q = qkv[unit, r * 256:n, lanes]
             k = jnp.concatenate([qkv[2 + unit, 0:n, lanes], bias_cols[0:n]], axis=1)
             v = jnp.concatenate([qkv[4 + unit, 0:n, lanes], jnp.ones((n, 128), bf16)], axis=1)
-            outs = []
+            queries, probs = [], []
             for half in range(2):
                 mine = (lane < 64) if half == 0 else (lane >= 64)
                 head = 2 * pair + half
                 pick = ((lane >= 3 * head) & (lane < 3 * head + 3)).astype(bf16)
-                query = jnp.concatenate([jnp.where(mine, q, jnp.zeros_like(q)), pick], axis=1)
-                scores = lax.dot_general(query, k, NT, preferred_element_type=f32)
+                queries.append(jnp.concatenate([jnp.where(mine, q, jnp.zeros_like(q)), pick], axis=1))
+            both = lax.dot_general(jnp.concatenate(queries, axis=0), k, NT, preferred_element_type=f32)
+            for half in range(2):
+                scores = both[half * 256:(half + 1) * 256]
                 last = jnp.maximum(jnp.minimum(scores[:, r * 256:], limits[0]), limits[1])
                 scores = jnp.concatenate([scores[:, :r * 256], last], axis=1) if r else last
-                probs = jnp.exp(scores - jnp.max(scores, axis=1, keepdims=True)).astype(bf16)
-                out = jnp.dot(probs, v, preferred_element_type=f32)
-                outs.append(out[:, :128] / out[:, 128:])
+                probs.append(jnp.exp(scores - jnp.max(scores, axis=1, keepdims=True)).astype(bf16))
+            out = jnp.dot(jnp.concatenate(probs, axis=0), v, preferred_element_type=f32)
+            outs = [out[half * 256:(half + 1) * 256, :128] / out[half * 256:(half + 1) * 256, 128:] for half in range(2)]
             ctx[unit, r * 256:n, lanes] = jnp.where(lane < 64, outs[0], outs[1]).astype(bf16)
         return carry
 
+    def leave(r):
+        return pltpu.make_async_copy(x.at[rows(r)], out_hbm.at[rows(r)], out_sem.at[r])
+
     def layer_body(layer, carry):
         base = layer * UNITS
 
-        def qkv_unit(j, carry):
-            torus.poll('qkv', layer, j)
-            scale = jnp.where(j < 2, 0.125, 1.0)
-            out = jnp.dot(a[...], weight(base + j), preferred_element_type=f32) + bias_rows[layer * 6 + j]
-            qkv[j] = (out * scale).astype(bf16)
-            return carry
-
-        lax.fori_loop(0, 6, qkv_unit, 0)
-        cache = pltpu.make_async_copy(qkv.at[2:6], cache_hbm.at[layer], cache_sem)
-        cache.start()
+        def project_in(half, width, start):
+            cols = pl.ds(start, width)
+            w = jnp.concatenate([blocks[base + 3 * half + kind, :, :, :, :, cols].reshape(1024, width) for kind in range(3)], axis=1)
+            out = jnp.dot(a[...], w, preferred_element_type=f32)
+            for kind in range(3):
+                slot = 2 * kind + half
+                piece = out[:, kind * width:(kind + 1) * width] + bias_rows[layer * 6 + slot, :, cols]
+                qkv[slot, :, cols] = (piece * 0.125 if kind == 0 else piece).astype(bf16)
+
+        caches = (pltpu.make_async_copy(keys, key_hbm.at[layer], key_sem),
+                  pltpu.make_async_copy(values, value_hbm.at[layer], value_sem))
 
         def attend_pair(pair, carry):
+            torus.poll('qkv', layer, pair)
+            half, second = lax.div(pair, 2), lax.rem(pair, 2)
+
+            @pl.when(layer == 0)
+            def _():
+                project_in(half, 128, pl.multiple_of(second * 128, 128))
+
+            @pl.when((layer == 1) & (second == 0))
+            def _():
+                project_in(half, 256, 0)
+
             torus.poll('attn', layer, pair)
-            return attention(pair, carry)
+            attention(layer, pair, carry)
+
+            @pl.when(second == 1)
+            def _():
+                keys[rows(half)] = qkv[2 + half].T
+                values[rows(half)] = qkv[4 + half].T
+            return carry
 
         lax.fori_loop(0, 4, attend_pair, 0)
+        for cache in caches:
+            cache.start()
 
         def send_after(kind, r):
             @pl.when(r > 0)
@@ -279,7 +332,7 @@
             both = bup_ref[:, cols].astype(f32)
             bias = jnp.where(layer == 0, both[0:1], both[1:2])
             out = jnp.dot(a[...], weight(base + 8 + j), preferred_element_type=f32) + bias
-            act[j] = jax.nn.gelu(out, approximate=True).astype(bf16)
+            act[j] = gelu(out).astype(bf16)
             return carry
 
         lax.fori_loop(0, 8, up_unit, 0)
@@ -308,7 +361,8 @@
         lax.fori_loop(0, 4, down_first, 0)
         lax.fori_loop(0, 4, down_next, 0)
         lax.fori_loop(0, 4, down_last, 0)
-        cache.wait()
+        for cache in caches:
+            cache.wait()
         exchange(layer, 1, 3).start()
 
         def finish(r, carry):
@@ -318,6 +372,10 @@
             @pl.when(layer == 0)
             def _():
                 a[rows(r)] = normalize(total, ln1s_ref[1:2].astype(f32), ln1b_ref[1:2].astype(f32))
+
+            @pl.when((layer == 1) & (r > 0))
+            def _():
+                leave(r - 1).start()
             return carry
 
         lax.fori_loop(0, 4, finish, 0)
@@ -331,16 +389,13 @@
         return carry
 
     lax.fori_loop(0, 2, layer_body, 0)
-    out = pltpu.make_async_copy(x, out_hbm, out_sem)
-    out.start()
-
-    def drain(chunk, carry):
+    leave(3).start()
+    for chunk in range(CHUNKS):
         for stage in range(STAGES):
-            torus.wait(send_sem, chunk, stage)
-        return carry
-
-    lax.fori_loop(0, CHUNKS, drain, 0)
-    out.wait()
+            if torus.used(chunk, stage):
+                torus.wait(send_sem, chunk, stage)
+    for r in range(4):
+        leave(r).wait()
 
 
 def run_layers(*operands):
@@ -348,9 +403,9 @@
     bf16, dma = jnp.bfloat16, pltpu.SemaphoreType.DMA
     return pl.pallas_call(
         layers_kernel,
-        out_shape=(jax.ShapeDtypeStruct((1024, 1024), bf16), jax.ShapeDtypeStruct((2, 4, 1024, 256), bf16)),
+        out_shape=(jax.ShapeDtypeStruct((1024, 1024), bf16),) + (jax.ShapeDtypeStruct((2, 512, 1024), bf16),) * 2,
         in_specs=[hbm] + [vmem] * 11 + [hbm] * 3,
-        out_specs=(hbm, hbm),
+        out_specs=(hbm,) * 3,
         scratch_shapes=[
             pltpu.VMEM((2 * UNITS, 4, 4, 4, 16, 256), bf16),
             pltpu.VMEM((1024, 1024), bf16),
@@ -364,6 +419,8 @@
             pltpu.VMEM((1024, 128), bf16),
             pltpu.VMEM((2, 256, 256), jnp.float32),
             pltpu.VMEM((12, 1, 256), jnp.float32),
+            pltpu.VMEM((512, 1024), bf16),
+            pltpu.VMEM((512, 1024), bf16),
             dma((CHUNKS, STAGES)),
             dma((CHUNKS, STAGES)),
             dma((2, 2, 4)),
@@ -372,31 +429,43 @@
             dma,
             dma,
             dma,
+            dma((4,)),
         ],
-        compiler_params=pltpu.CompilerParams(collective_id=0, has_side_effects=True, vmem_limit_bytes=67043328),
+        compiler_params=pltpu.CompilerParams(collective_id=0, has_side_effects=True, vmem_limit_bytes=58*2**20),
         name='two_layers',
     )(*operands)
 
 
-def finish_kernel(x_ref, key_ref, value_ref, out_ref, key_out, value_out):
-    out_ref[...] = x_ref[...]
-    key_out[0] = key_ref[0, 0].T
-    value_out[0] = value_ref[0, 0].T
-
-
-def finish_outputs(x, cache):
-    bf16 = jnp.bfloat16
-    across = pl.BlockSpec((1, 128, 1024), lambda i: (i // 4, i % 4, 0))
+PIECES = 4
+
+
+def pass_kernel(*refs):
+    sources, targets, (held, in_sem, out_sem) = refs[:3], refs[3:6], refs[6:]
+    size = 1024 // PIECES
+    views = [(k * PIECES + p, sources[k].at[p * size:(p + 1) * size], targets[k].at[p * size:(p + 1) * size])
+             for p in range(PIECES) for k in range(3)]
+    into = [pltpu.make_async_copy(src, held.at[n], in_sem.at[n]) for n, src, _ in views]
+    out = [pltpu.make_async_copy(held.at[n], dst, out_sem.at[n]) for n, _, dst in views]
+    for copy in into:
+        copy.start()
+    for first, second in zip(into, out):
+        first.wait()
+        second.start()
+    for copy in out:
+        copy.wait()
+
+
+def pass_on(*arrays):
+    shape = jax.ShapeDtypeStruct((1024, 1024), jnp.bfloat16)
+    dma = pltpu.SemaphoreType.DMA
     return pl.pallas_call(
-        finish_kernel,
-        grid=(8,),
-        out_shape=(jax.ShapeDtypeStruct(x.shape, bf16),) + (jax.ShapeDtypeStruct((2, 512, 1024), bf16),) * 2,
-        in_specs=[pl.BlockSpec((128, 1024), lambda i: (i, 0)),
-                  pl.BlockSpec((1, 1, 1024, 128), lambda i: (i // 4, (i % 4) // 2, 0, i % 2)),
-                  pl.BlockSpec((1, 1, 1024, 128), lambda i: (i // 4, 2 + (i % 4) // 2, 0, i % 2))],
-        out_specs=(pl.BlockSpec((128, 1024), lambda i: (i, 0)), across, across),
-        name='finish_outputs',
-    )(x, cache, cache)
+        pass_kernel,
+        out_shape=(shape,) * 3,
+        in_specs=[pl.BlockSpec(memory_space=pl.ANY)] * 3,
+        out_specs=(pl.BlockSpec(memory_space=pl.ANY),) * 3,
+        scratch_shapes=[pltpu.VMEM((3 * PIECES, 1024 // PIECES, 1024), jnp.bfloat16), dma((3 * PIECES,)), dma((3 * PIECES,))],
+        name='pass_on',
+    )(*arrays)
 
 
 def solution(mesh):
@@ -408,11 +477,11 @@
         n_layers, _, local_heads, _, head_dim = w_qkv.shape
         slopes = np.zeros((tp_size, 128), np.float32)
         slopes[:, :3 * local_heads] = np.repeat(alibi_slopes(local_heads * tp_size).reshape(tp_size, local_heads), 3, axis=1)
-        out, cache = run_layers(
+        out, keys, values = run_layers(
             hidden.reshape(hidden.shape[1:]), attn_mask, slopes, ln1_scale, ln1_bias, ln2_scale, ln2_bias,
             b_qkv.transpose(0, 2, 1, 3), b_out, b_up, b_down, w_out.transpose(0, 1, 3, 2),
             w_qkv.transpose(0, 1, 3, 2, 4).reshape(n_layers, 16, -1), w_up, w_down.transpose(0, 2, 1))
-        out, keys, values = finish_outputs(out, cache)
+        out, keys, values = pass_on(out, keys.reshape(1024, 1024), values.reshape(1024, 1024))
         caches = [c.reshape(n_layers, 1, local_heads, head_dim, 1024).transpose(0, 1, 4, 2, 3) for c in (keys, values)]
         return out.reshape(hidden.shape), *caches
 

time: 134 us -> 127 us (0.948)
  Pallas kernels: 132 us -> 124 us
    pallas_call x1, Pallas kernels: 124 us -> 119 us  [run_layers(): pl.pallas_call(layers_kernel, out_shape=(jax.ShapeDtypeStruct((1024, 1024...]
    pallas_call x1, Pallas kernels: 7.95 us -> 5.46 us  [pass_on(): pl.pallas_call(pass_kernel, out_shape=(shape,) * 3, in_specs=[pl.BlockSpe...]
where the time goes in v4:
time: 127 us
  Pallas kernels  124 us (98%)
  local copies, waits for them, and re-layouts  1.76 us (1%)
    pallas_call x1, Pallas kernels, run_layers(): pl.pallas_call(layers_kernel, out_shape=(jax.ShapeDtypeStruct((1024, 1024...  119 us
    pallas_call x1, Pallas kernels, pass_on(): pl.pallas_call(pass_kernel, out_shape=(shape,) * 3, in_specs=[pl.BlockSpe...  5.46 us

profile of v4, /device:TPU:1, one launch (start us, length us, event | category | flops | bytes accessed | tf_op | source)
XLA Modules:
  0.0 126.9 jit_solution(1406790160116056967)
XLA Ops:
  0.6 1.8 %reshape.28.wqkv_hbm = bf16[2,16,1536]{2,1,0:T(8,128)(2,1)} reshape(bf16[2,16,3,8,64]{4,3,2,1,0:T(8,128)(2,1)} %bitcast.23) | data formatting | bytes 196608 | tf_op jit(solution)/shard_map/reshape | solution.py:483
  2.4 119.0 %two_layers.1 = (bf16[1024,1024]{1,0:T(8,128)(2,1)}, bf16[2,512,1024]{2,1,0:T(8,128)(2,1)}, bf16[2,512,1024]{2,1,0:T(8,128)(2,1)}) custom-call(bf16[1024,1024]{1,0:T(8,128)(2,1)} %bitcast.22, s32[1,1024]{1,0:T(1,128)} %mask_ref.1, f32[2,128]{1,0:T(2,128)} %constant.2.clone.slope_ref, bf16[2,1024]{1,0:T(2,128)(2,1)} %ln1s_ref.1, bf16[2,1024]{1,0:T(2,128)(2,1)} %ln1b_ref.1, ...), custom_call_target="tpu_custom_call" | custom-call | tf_op jit(solution)/shard_map/two_layers/pallas_call | solution.py:404
  121.4 5.5 %pass_on.1 = (bf16[1024,1024]{1,0:T(8,128)(2,1)}, bf16[1024,1024]{1,0:T(8,128)(2,1)}, bf16[1024,1024]{1,0:T(8,128)(2,1)}) custom-call(bf16[1024,1024]{1,0:T(8,128)(2,1)} %get-tuple-element.9.refs_0_, bf16[1024,1024]{1,0:T(8,128)(2,1)} %bitcast.20, bf16[1024,1024]{1,0:T(8,128)(2,1)} %bitcast.21), custom_call_target="tpu_custom_call" | custom-call | tf_op jit(solution)/shard_map/pass_on/pallas_call | solution.py:461

commit v5 on v4

--- a/solution.py
+++ b/solution.py
@@ -18,15 +18,15 @@
 STAGES = 6
 SCHEDULE = {
     'head': ((0, 0, ((0, 0), (1, 0), (2, 0), (3, 0), (4, 0), (5, 0), (6, 0), (7, 0), (8, 0), (9, 0), (10, 0), (11, 0), (12, 0), (13, 0), (14, 0), (15, 0), (16, 0), (17, 0))),),
-    'qkv': ((0, 0, ((0, 1), (0, 2), (0, 3), (9, 1), (1, 1), (2, 1), (3, 1), (4, 1), (5, 1), (6, 1), (7, 1), (8, 1), (10, 1), (11, 1), (12, 1), (13, 1), (14, 1), (15, 1), (16, 1), (9, 2), (1, 2), (2, 2), (7, 2), (0, 4), (9, 3), (3, 2), (4, 2), (2, 3), (7, 3), (1, 3), (5, 2), (0, 5), (6, 2), (3, 3), (4, 3), (8, 2), (7, 4), (0, 6), (1, 4))), (0, 1, ((1, 5), (2, 5), (4, 4), (1, 6), (5, 4))), (0, 2, ((2, 6), (4, 5))), (0, 3, ((3, 6),)), (1, 0, ((10, 6), (11, 5))), (1, 2, ((11, 6), (13, 5)))),
-    'attn': ((0, 0, ((2, 4), (5, 3), (6, 3), (3, 4))), (0, 1, ((3, 5), (6, 4))), (0, 2, ((7, 5), (8, 3), (9, 4))), (0, 3, ((5, 5), (10, 2), (6, 5))), (1, 0, ((14, 4),)), (1, 1, ((12, 5), (15, 4))), (1, 2, ((16, 4),)), (1, 3, ((14, 5), (17, 3)))),
-    'proj': ((0, 0, ((4, 6),)), (0, 2, ((8, 4),)), (1, 0, ((12, 6), (15, 5)))),
-    'mid': ((0, 1, ((9, 5),)), (0, 3, ((11, 2),)), (1, 1, ((16, 5),))),
-    'up': ((0, 0, ((10, 3), (12, 2))), (0, 1, ((5, 6), (13, 2))), (0, 2, ((14, 2), (15, 2))), (0, 3, ((16, 2),)), (0, 4, ((6, 6), (8, 5))), (0, 5, ((17, 1),)), (0, 6, ((11, 3),)), (0, 7, ((7, 6), (10, 4))), (1, 0, ((17, 4),)), (1, 1, ((13, 6),)), (1, 4, ((14, 6),)), (1, 7, ((15, 6),))),
-    'd0': ((0, 2, ((12, 3), (13, 3))), (0, 3, ((14, 3),)), (1, 0, ((17, 5),))),
-    'd1': ((0, 0, ((8, 6), (15, 3), (16, 3))), (0, 2, ((11, 4),)), (1, 0, ((16, 6),))),
-    'd2': ((0, 0, ((9, 6), (17, 2))), (0, 2, ((10, 5),)), (0, 3, ((12, 4),)), (1, 0, ((17, 6),))),
-    'fin': ((0, 2, ((13, 4),)),),
+    'norm': ((0, 2, ((1, 1), (2, 1), (3, 1), (4, 1))), (0, 3, ((0, 1), (0, 2), (5, 1), (6, 1), (7, 1), (8, 1), (9, 1)))),
+    'qkv': ((0, 0, ((0, 3), (1, 2), (2, 2), (3, 2), (4, 2), (5, 2), (0, 4), (1, 3), (2, 3), (3, 3), (4, 3), (5, 3), (0, 5), (1, 4), (2, 4), (3, 4), (5, 4), (0, 6))), (0, 1, ((2, 5), (4, 4), (5, 5), (3, 5), (1, 6))), (0, 2, ((2, 6), (4, 5), (9, 2))), (0, 3, ((3, 6), (7, 3), (8, 3))), (1, 0, ((12, 4), (10, 6))), (1, 2, ((12, 5), (13, 4), (11, 6), (14, 4)))),
+    'attn': ((0, 0, ((1, 5),)), (0, 1, ((6, 2), (7, 2), (8, 2))), (0, 2, ((10, 1), (11, 1), (12, 1), (13, 1), (14, 1), (6, 3), (15, 1), (16, 1), (17, 1))), (0, 3, ((6, 4), (9, 3), (10, 2))), (1, 0, ((13, 3), (14, 3), (15, 3), (16, 3), (17, 3))), (1, 1, ((11, 5),)), (1, 3, ((15, 4),))),
+    'proj': ((0, 0, ((4, 6), (7, 4))), (1, 0, ((12, 6), (13, 5)))),
+    'mid': ((0, 0, ((8, 4),)), (1, 0, ((14, 5), (16, 4)))),
+    'up': ((0, 0, ((6, 5),)), (0, 1, ((5, 6), (9, 4))), (0, 4, ((7, 5), (10, 3), (8, 5), (6, 6))), (0, 6, ((11, 2),)), (0, 7, ((12, 2), (9, 5), (7, 6))), (1, 0, ((15, 5),)), (1, 1, ((13, 6), (17, 4))), (1, 4, ((14, 6),)), (1, 5, ((16, 5),)), (1, 7, ((15, 6),))),
+    'd1': ((0, 0, ((10, 4), (8, 6))), (0, 1, ((11, 3),)), (0, 2, ((12, 3), (13, 2))), (0, 3, ((14, 2),)), (1, 0, ((17, 5), (16, 6)))),
+    'd2': ((0, 0, ((9, 6), (15, 2))), (0, 1, ((16, 2),)), (0, 2, ((17, 2),)), (0, 3, ((10, 5),)), (1, 0, ((17, 6),))),
+    'fin': ((0, 0, ((11, 4),)),),
 }
 NT = (((1,), (1,)), ((), ()))
 ORDERS = (('x', 'y', 'z'), ('y', 'z', 'x'), ('z', 'x', 'y'))
@@ -59,13 +59,15 @@
     def view(self, unit, where, cols=slice(0, 256)):
         return self.blocks.at[unit, where['z'], where['y'], where['x'], :, cols]
 
-    def barrier(self):
+    def greet(self):
         sem = pltpu.get_barrier_semaphore()
         for ax in 'zyx':
             for dev in (self.left[ax], self.right[ax], self.across[ax]):
                 pl.semaphore_signal(sem, inc=1, device_id={'wg': dev}, device_id_type=MESH)
         pl.semaphore_signal(sem, inc=1, device_id={'tp': 1 - lax.axis_index('tp')}, device_id_type=MESH)
-        pl.semaphore_wait(sem, 10)
+
+    def meet(self):
+        pl.semaphore_wait(pltpu.get_barrier_semaphore(), 10)
 
     def part(self, chunk):
         if chunk < HALVES:
@@ -153,7 +155,7 @@
 
 
 def layers_kernel(x_hbm, mask_ref, slope_ref, ln1s_ref, ln1b_ref, ln2s_ref, ln2b_ref, bqkv_ref, bout_ref, bup_ref, bdown_ref,
-                  wout_ref, wqkv_hbm, wup_hbm, wdown_hbm, out_hbm, key_hbm, value_hbm,
+                  wout_ref, wqkv_ref, wup_hbm, wdown_hbm, out_hbm, key_hbm, value_hbm,
                   blocks, x, a, qkv, ctx, act, acc, part, other, bias_cols, limits, bias_rows, keys, values,
                   send_sem, recv_sem, part_send, part_recv, own_sem, x_sem, key_sem, value_sem, out_sem):
     f32, bf16 = jnp.float32, jnp.bfloat16
@@ -161,12 +163,11 @@
     partner = {'tp': 1 - lax.axis_index('tp')}
     mine = (torus.pos['z'], torus.pos['y'], torus.pos['x'])
     own = []
+    torus.greet()
     for layer in range(2):
-        for first, weights, count in ((0, wqkv_hbm, 6), (8, wup_hbm, 8), (16, wdown_hbm, 8)):
-            for j in range(count):
-                at = (j % 3) * 512 + (j // 3) * 256 if first == 0 else j * 256
-                own.append(pltpu.make_async_copy(weights.at[layer, :, at:at + 256],
-                                                 blocks.at[(layer * UNITS + first + j,) + mine], own_sem))
+        for first, weights in ((8, wup_hbm), (16, wdown_hbm)):
+            own += [pltpu.make_async_copy(weights.at[layer, :, j * 256:(j + 1) * 256],
+                                          blocks.at[(layer * UNITS + first + j,) + mine], own_sem) for j in range(8)]
     for copy in own:
         copy.start()
     x_in = pltpu.make_async_copy(x_hbm, x, x_sem)
@@ -175,8 +176,13 @@
         flat = jnp.concatenate([wout_ref[layer, head] for head in range(8)], axis=1)
         for j in range(2):
             blocks[(layer * UNITS + 6 + j,) + mine] = flat[:, j * 256:(j + 1) * 256]
-    torus.barrier()
-    whole = blocks.at[0:44, 0, 0, 0]
+    for layer in range(2):
+        for half in range(2):
+            for kind in range(3):
+                heads = [wqkv_ref[layer, :, kind, h, :] for h in range(4 * half, 4 * half + 4)]
+                blocks[(layer * UNITS + 3 * half + kind,) + mine] = jnp.concatenate(heads, axis=1)
+    torus.meet()
+    whole = blocks.at[0:32, 0, 0, 0]
     pltpu.make_async_copy(whole, whole, own_sem).wait()
     zero = jnp.int32(0)
     torus.poll('head', zero, zero)
@@ -291,16 +297,9 @@
 
             torus.poll('attn', layer, pair)
             attention(layer, pair, carry)
-
-            @pl.when(second == 1)
-            def _():
-                keys[rows(half)] = qkv[2 + half].T
-                values[rows(half)] = qkv[4 + half].T
             return carry
 
         lax.fori_loop(0, 4, attend_pair, 0)
-        for cache in caches:
-            cache.start()
 
         def send_after(kind, r):
             @pl.when(r > 0)
@@ -316,7 +315,19 @@
             return carry
 
         lax.fori_loop(0, 4, project, 0)
-        exchange(layer, 0, 3).start()
+
+        def turn(half, carry):
+            keys[rows(half)] = qkv[2 + half].T
+            values[rows(half)] = qkv[4 + half].T
+
+            @pl.when(half == 0)
+            def _():
+                exchange(layer, 0, 3).start()
+            return carry
+
+        lax.fori_loop(0, 2, turn, 0)
+        for cache in caches:
+            cache.start()
 
         def second_norm(r, carry):
             torus.poll('mid', layer, r)
@@ -342,14 +353,9 @@
             w = jnp.concatenate([weight(base + 16 + j) for j in units], axis=1)
             return lax.dot_general(h, w, NT, preferred_element_type=f32)
 
-        def down_first(r, carry):
-            torus.poll('d0', layer, r)
-            acc[rows(r)] = down_product(r, (0, 1))
-            return carry
-
         def down_next(r, carry):
             torus.poll('d1', layer, r)
-            acc[rows(r)] += down_product(r, (2, 3, 4))
+            acc[rows(r)] = down_product(r, (0, 1, 2, 3, 4))
             return carry
 
         def down_last(r, carry):
@@ -358,13 +364,19 @@
             send_after(1, r)
             return carry
 
-        lax.fori_loop(0, 4, down_first, 0)
         lax.fori_loop(0, 4, down_next, 0)
         lax.fori_loop(0, 4, down_last, 0)
         for cache in caches:
             cache.wait()
         exchange(layer, 1, 3).start()
 
+        @pl.when(layer == 1)
+        def _():
+            for chunk in range(CHUNKS):
+                for stage in range(STAGES):
+                    if torus.used(chunk, stage):
+                        torus.wait(send_sem, chunk, stage)
+
         def finish(r, carry):
             torus.poll('fin', layer, r)
             total = residual(layer, 1, r, row_of(bdown_ref, layer))
@@ -390,10 +402,6 @@
 
     lax.fori_loop(0, 2, layer_body, 0)
     leave(3).start()
-    for chunk in range(CHUNKS):
-        for stage in range(STAGES):
-            if torus.used(chunk, stage):
-                torus.wait(send_sem, chunk, stage)
     for r in range(4):
         leave(r).wait()
 
@@ -404,7 +412,7 @@
     return pl.pallas_call(
         layers_kernel,
         out_shape=(jax.ShapeDtypeStruct((1024, 1024), bf16),) + (jax.ShapeDtypeStruct((2, 512, 1024), bf16),) * 2,
-        in_specs=[hbm] + [vmem] * 11 + [hbm] * 3,
+        in_specs=[hbm] + [vmem] * 12 + [hbm] * 2,
         out_specs=(hbm,) * 3,
         scratch_shapes=[
             pltpu.VMEM((2 * UNITS, 4, 4, 4, 16, 256), bf16),
@@ -480,7 +488,7 @@
         out, keys, values = run_layers(
             hidden.reshape(hidden.shape[1:]), attn_mask, slopes, ln1_scale, ln1_bias, ln2_scale, ln2_bias,
             b_qkv.transpose(0, 2, 1, 3), b_out, b_up, b_down, w_out.transpose(0, 1, 3, 2),
-            w_qkv.transpose(0, 1, 3, 2, 4).reshape(n_layers, 16, -1), w_up, w_down.transpose(0, 2, 1))
+            w_qkv.transpose(0, 1, 3, 2, 4), w_up, w_down.transpose(0, 2, 1))
         out, keys, values = pass_on(out, keys.reshape(1024, 1024), values.reshape(1024, 1024))
         caches = [c.reshape(n_layers, 1, local_heads, head_dim, 1024).transpose(0, 1, 4, 2, 3) for c in (keys, values)]
         return out.reshape(hidden.shape), *caches

time: 127 us -> 124 us (0.976)
  local copies, waits for them, and re-layouts: 1.76 us -> 0 us
    reshape x1 -> x0, local copies, waits for them, and re-layouts: 1.76 us -> none  [device_fn(): w_qkv.transpose(0, 1, 3, 2, 4).reshape(n_layers, 16, -1)]
    pallas_call x1, Pallas kernels: 119 us -> 118 us  [run_layers(): pl.pallas_call(layers_kernel, out_shape=(jax.ShapeDtypeStruct((1024, 1024...]
where the time goes in v5:
time: 124 us
  Pallas kernels  123 us (99%)
    pallas_call x1, Pallas kernels, run_layers(): pl.pallas_call(layers_kernel, out_shape=(jax.ShapeDtypeStruct((1024, 1024...  118 us
    pallas_call x1, Pallas kernels, pass_on(): pl.pallas_call(pass_kernel, out_shape=(shape,) * 3, in_specs=[pl.BlockSpe...  5.46 us

profile of v5, /device:TPU:1, one launch (start us, length us, event | category | flops | bytes accessed | tf_op | source)
XLA Modules:
  0.0 123.9 jit_solution(3144806322942084220)
XLA Ops:
  0.6 117.7 %two_layers.1 = (bf16[1024,1024]{1,0:T(8,128)(2,1)}, bf16[2,512,1024]{2,1,0:T(8,128)(2,1)}, bf16[2,512,1024]{2,1,0:T(8,128)(2,1)}) custom-call(bf16[1024,1024]{1,0:T(8,128)(2,1)} %bitcast.20, s32[1,1024]{1,0:T(1,128)} %mask_ref.1, f32[2,128]{1,0:T(2,128)} %constant.2.clone.slope_ref, bf16[2,1024]{1,0:T(2,128)(2,1)} %ln1s_ref.1, bf16[2,1024]{1,0:T(2,128)(2,1)} %ln1b_ref.1, ...), custom_call_target="tpu_custom_call" | custom-call | tf_op jit(solution)/shard_map/two_layers/pallas_call | solution.py:412
  118.3 5.5 %pass_on.1 = (bf16[1024,1024]{1,0:T(8,128)(2,1)}, bf16[1024,1024]{1,0:T(8,128)(2,1)}, bf16[1024,1024]{1,0:T(8,128)(2,1)}) custom-call(bf16[1024,1024]{1,0:T(8,128)(2,1)} %get-tuple-element.9.refs_0_, bf16[1024,1024]{1,0:T(8,128)(2,1)} %bitcast.18, bf16[1024,1024]{1,0:T(8,128)(2,1)} %bitcast.19), custom_call_target="tpu_custom_call" | custom-call | tf_op jit(solution)/shard_map/pass_on/pallas_call | solution.py:469

commit v6 on v5

--- a/solution.py
+++ b/solution.py
@@ -14,19 +14,19 @@
 UNITS = 24
 HALVES = 4
 CHUNKS = 18
-DIRECT = (0,)
+DIRECT = (0, 1)
 STAGES = 6
 SCHEDULE = {
     'head': ((0, 0, ((0, 0), (1, 0), (2, 0), (3, 0), (4, 0), (5, 0), (6, 0), (7, 0), (8, 0), (9, 0), (10, 0), (11, 0), (12, 0), (13, 0), (14, 0), (15, 0), (16, 0), (17, 0))),),
-    'norm': ((0, 2, ((1, 1), (2, 1), (3, 1), (4, 1))), (0, 3, ((0, 1), (0, 2), (5, 1), (6, 1), (7, 1), (8, 1), (9, 1)))),
-    'qkv': ((0, 0, ((0, 3), (1, 2), (2, 2), (3, 2), (4, 2), (5, 2), (0, 4), (1, 3), (2, 3), (3, 3), (4, 3), (5, 3), (0, 5), (1, 4), (2, 4), (3, 4), (5, 4), (0, 6))), (0, 1, ((2, 5), (4, 4), (5, 5), (3, 5), (1, 6))), (0, 2, ((2, 6), (4, 5), (9, 2))), (0, 3, ((3, 6), (7, 3), (8, 3))), (1, 0, ((12, 4), (10, 6))), (1, 2, ((12, 5), (13, 4), (11, 6), (14, 4)))),
-    'attn': ((0, 0, ((1, 5),)), (0, 1, ((6, 2), (7, 2), (8, 2))), (0, 2, ((10, 1), (11, 1), (12, 1), (13, 1), (14, 1), (6, 3), (15, 1), (16, 1), (17, 1))), (0, 3, ((6, 4), (9, 3), (10, 2))), (1, 0, ((13, 3), (14, 3), (15, 3), (16, 3), (17, 3))), (1, 1, ((11, 5),)), (1, 3, ((15, 4),))),
-    'proj': ((0, 0, ((4, 6), (7, 4))), (1, 0, ((12, 6), (13, 5)))),
-    'mid': ((0, 0, ((8, 4),)), (1, 0, ((14, 5), (16, 4)))),
-    'up': ((0, 0, ((6, 5),)), (0, 1, ((5, 6), (9, 4))), (0, 4, ((7, 5), (10, 3), (8, 5), (6, 6))), (0, 6, ((11, 2),)), (0, 7, ((12, 2), (9, 5), (7, 6))), (1, 0, ((15, 5),)), (1, 1, ((13, 6), (17, 4))), (1, 4, ((14, 6),)), (1, 5, ((16, 5),)), (1, 7, ((15, 6),))),
-    'd1': ((0, 0, ((10, 4), (8, 6))), (0, 1, ((11, 3),)), (0, 2, ((12, 3), (13, 2))), (0, 3, ((14, 2),)), (1, 0, ((17, 5), (16, 6)))),
-    'd2': ((0, 0, ((9, 6), (15, 2))), (0, 1, ((16, 2),)), (0, 2, ((17, 2),)), (0, 3, ((10, 5),)), (1, 0, ((17, 6),))),
-    'fin': ((0, 0, ((11, 4),)),),
+    'norm': ((0, 3, ((2, 1), (0, 1), (0, 2), (3, 1), (4, 1), (5, 1), (1, 1), (1, 2))),),
+    'qkv': ((0, 0, ((0, 3), (6, 1), (7, 1), (8, 1), (9, 1), (10, 1), (11, 1), (12, 1), (13, 1), (14, 1), (15, 1), (16, 1), (2, 2), (3, 2), (4, 2), (5, 2), (0, 4), (6, 2), (8, 2), (16, 2), (3, 3), (1, 3), (1, 4), (0, 5), (2, 3), (4, 3), (5, 3), (7, 2), (8, 3), (6, 3), (16, 3), (9, 2), (1, 5), (3, 4), (0, 6), (10, 2))), (0, 1, ((1, 6),)), (0, 2, ((2, 5), (4, 5), (5, 5), (6, 4), (2, 6))), (0, 3, ((3, 6),)), (1, 0, ((10, 6), (11, 5))), (1, 2, ((13, 5), (11, 6)))),
+    'attn': ((0, 0, ((2, 4), (4, 4))), (0, 1, ((3, 5), (5, 4))), (0, 2, ((7, 3), (8, 4))), (0, 3, ((9, 3), (10, 3), (11, 2), (12, 2), (13, 2))), (1, 0, ((14, 3), (15, 3), (16, 5))), (1, 1, ((12, 5), (17, 2))), (1, 2, ((14, 4),)), (1, 3, ((15, 4),))),
+    'proj': ((0, 0, ((4, 6),)), (0, 1, ((6, 5),)), (1, 0, ((12, 6),)), (1, 3, ((17, 3),))),
+    'mid': ((0, 0, ((7, 4),)), (0, 2, ((8, 5),)), (1, 1, ((14, 5),))),
+    'up': ((0, 0, ((9, 4),)), (0, 1, ((5, 6),)), (0, 3, ((10, 4),)), (0, 4, ((6, 6),)), (0, 6, ((7, 5),)), (0, 7, ((9, 5), (10, 5), (11, 3), (12, 3), (13, 3), (14, 2), (7, 6), (15, 2))), (1, 0, ((15, 5), (17, 4))), (1, 1, ((13, 6),)), (1, 4, ((14, 6),)), (1, 7, ((15, 6),))),
+    'd1': ((0, 0, ((8, 6), (16, 4))), (0, 2, ((17, 1), (11, 4))), (1, 0, ((16, 6), (17, 5)))),
+    'd2': ((0, 0, ((9, 6),)), (0, 2, ((12, 4),)), (1, 0, ((17, 6),))),
+    'fin': ((0, 0, ((13, 4),)),),
 }
 NT = (((1,), (1,)), ((), ()))
 ORDERS = (('x', 'y', 'z'), ('y', 'z', 'x'), ('z', 'x', 'y'))
@@ -243,26 +243,43 @@
     def attention(layer, pair, carry):
         unit, lanes = lax.div(pair, 2), pl.ds(pl.multiple_of(lax.rem(pair, 2) * 128, 128), 128)
         lane = lax.broadcasted_iota(jnp.int32, (256, 128), 1)
-        for r in range(4):
+        def score(r):
             n = (r + 1) * 256
             q = qkv[unit, r * 256:n, lanes]
             k = jnp.concatenate([qkv[2 + unit, 0:n, lanes], bias_cols[0:n]], axis=1)
-            v = jnp.concatenate([qkv[4 + unit, 0:n, lanes], jnp.ones((n, 128), bf16)], axis=1)
-            queries, probs = [], []
+            queries = []
             for half in range(2):
                 mine = (lane < 64) if half == 0 else (lane >= 64)
                 head = 2 * pair + half
                 pick = ((lane >= 3 * head) & (lane < 3 * head + 3)).astype(bf16)
                 queries.append(jnp.concatenate([jnp.where(mine, q, jnp.zeros_like(q)), pick], axis=1))
-            both = lax.dot_general(jnp.concatenate(queries, axis=0), k, NT, preferred_element_type=f32)
+            return lax.dot_general(jnp.concatenate(queries, axis=0), k, NT, preferred_element_type=f32)
+
+        def weigh(r, both):
+            probs = []
             for half in range(2):
                 scores = both[half * 256:(half + 1) * 256]
                 last = jnp.maximum(jnp.minimum(scores[:, r * 256:], limits[0]), limits[1])
                 scores = jnp.concatenate([scores[:, :r * 256], last], axis=1) if r else last
                 probs.append(jnp.exp(scores - jnp.max(scores, axis=1, keepdims=True)).astype(bf16))
-            out = jnp.dot(jnp.concatenate(probs, axis=0), v, preferred_element_type=f32)
+            return jnp.concatenate(probs, axis=0)
+
+        def mix(r, probs):
+            n = (r + 1) * 256
+            v = jnp.concatenate([qkv[4 + unit, 0:n, lanes], jnp.ones((n, 128), bf16)], axis=1)
+            out = jnp.dot(probs, v, preferred_element_type=f32)
             outs = [out[half * 256:(half + 1) * 256, :128] / out[half * 256:(half + 1) * 256, 128:] for half in range(2)]
             ctx[unit, r * 256:n, lanes] = jnp.where(lane < 64, outs[0], outs[1]).astype(bf16)
+
+        order = (3, 2, 1, 0)
+        scores, probs = {3: score(3)}, {}
+        for n, r in enumerate(order):
+            if n < 3:
+                scores[r - 1] = score(r - 1)
+            probs[r] = weigh(r, scores.pop(r))
+            if n > 0:
+                mix(r + 1, probs.pop(r + 1))
+        mix(0, probs.pop(0))
         return carry
 
     def leave(r):
@@ -439,7 +456,7 @@
             dma,
             dma((4,)),
         ],
-        compiler_params=pltpu.CompilerParams(collective_id=0, has_side_effects=True, vmem_limit_bytes=58*2**20),
+        compiler_params=pltpu.CompilerParams(collective_id=0, has_side_effects=True, vmem_limit_bytes=67043328),
         name='two_layers',
     )(*operands)
 

time: 124 us -> 122 us (0.984)
  Pallas kernels: 123 us -> 121 us
    pallas_call x1, Pallas kernels: 118 us -> 116 us  [run_layers(): pl.pallas_call(layers_kernel, out_shape=(jax.ShapeDtypeStruct((1024, 1024...]
where the time goes in v6:
time: 122 us
  Pallas kernels  121 us (99%)
    pallas_call x1, Pallas kernels, run_layers(): pl.pallas_call(layers_kernel, out_shape=(jax.ShapeDtypeStruct((1024, 1024...  116 us
    pallas_call x1, Pallas kernels, pass_on(): pl.pallas_call(pass_kernel, out_shape=(shape,) * 3, in_specs=[pl.BlockSpe...  5.46 us

profile of v6, /device:TPU:1, one launch (start us, length us, event | category | flops | bytes accessed | tf_op | source)
XLA Modules:
  0.0 121.8 jit_solution(13722451399105934180)
XLA Ops:
  0.6 115.7 %two_layers.1 = (bf16[1024,1024]{1,0:T(8,128)(2,1)}, bf16[2,512,1024]{2,1,0:T(8,128)(2,1)}, bf16[2,512,1024]{2,1,0:T(8,128)(2,1)}) custom-call(bf16[1024,1024]{1,0:T(8,128)(2,1)} %bitcast.20, s32[1,1024]{1,0:T(1,128)} %mask_ref.1, f32[2,128]{1,0:T(2,128)} %constant.2.clone.slope_ref, bf16[2,1024]{1,0:T(2,128)(2,1)} %ln1s_ref.1, bf16[2,1024]{1,0:T(2,128)(2,1)} %ln1b_ref.1, ...), custom_call_target="tpu_custom_call" | custom-call | tf_op jit(solution)/shard_map/two_layers/pallas_call | solution.py:429
  116.4 5.5 %pass_on.1 = (bf16[1024,1024]{1,0:T(8,128)(2,1)}, bf16[1024,1024]{1,0:T(8,128)(2,1)}, bf16[1024,1024]{1,0:T(8,128)(2,1)}) custom-call(bf16[1024,1024]{1,0:T(8,128)(2,1)} %get-tuple-element.9.refs_0_, bf16[1024,1024]{1,0:T(8,128)(2,1)} %bitcast.18, bf16[1024,1024]{1,0:T(8,128)(2,1)} %bitcast.19), custom_call_target="tpu_custom_call" | custom-call | tf_op jit(solution)/shard_map/pass_on/pallas_call | solution.py:486
